TPU v7x, 32 devices: a whole 2x2x4 slice. The times are simulated.
32 devices in a mesh: tm: 8 (over z, x), rows: 4 (over y, core).
Axes of the slice: x: 2, y: 2, z: 4, core: 2. Of those that a mesh axis runs over, the one named last changes fastest.
Arguments:
- initial_warmth: float32 [1024, 1024], P('rows'), may hold values from -6 to 6
- pattern_choice: int32 [16, 8, 8], P('tm'), may hold values from 0 to 7
- dissipation_tables: float32 [8, 128, 128], replicated, may hold values from -6 to 6
- material_label: int32 [8, 8], replicated, may hold values from 0 to 3
- intercept_kappa: float32 [4], replicated, may hold values from 4 to 8
- sensitivity_coef: float32 [4], replicated, may hold values from -0.5 to 0.5
Outputs:
- warmth_trajectory: float32 [16, 1024, 1024], P('tm', 'rows')
All inputs are finite; a program needn't handle non-finite values.
Results may differ from a plain program's by a relative error of at most 0.0003.
Values sent between devices are 32-bit elements; how exact they have to be, the bound alone decides.
A program may use at most 128 MiB of HBM per device.

v0:
```python
import math

import jax
import jax.numpy as jnp
import numpy as np
from jax import lax
from jax.experimental import pallas as pl
from jax.experimental.pallas import tpu as pltpu
from jax.sharding import PartitionSpec as P

TILE = 128
ITERS = 2
TIMESTEP_SIZE = 2.0
ALPHA = 0.05
CROSS_WEIGHT = 1.0 / 64.0
F32 = jnp.float32
BF16 = jnp.bfloat16


def extended(block, axis, dim):
    count = lax.axis_size(axis)
    forward = [(i, i + 1) for i in range(count - 1)]
    backward = [(target, source) for source, target in forward]
    low = lax.ppermute(
        lax.slice_in_dim(block, block.shape[dim] - 1, None, axis=dim), axis, forward
    )
    high = lax.ppermute(lax.slice_in_dim(block, 0, 1, axis=dim), axis, backward)
    return jnp.concatenate([low, block, high], axis=dim)


def cosine_table(length):
    modes = np.arange(length, dtype=np.int64)[:, None]
    cells = np.arange(length, dtype=np.int64)[None, :]
    phase = modes * (2 * cells + 1) % (4 * length)
    return np.cos(phase * (math.pi / (2 * length)))


def two_parts(table):
    high = np.asarray(table, dtype=np.float32).astype(BF16)
    low = (table - high.astype(np.float64)).astype(np.float32).astype(BF16)
    return jnp.asarray(high), jnp.asarray(low)


def split(values):
    high = values.astype(BF16)
    return high, (values - high.astype(F32)).astype(BF16)


def mul(left, right):
    return jnp.dot(left, right, preferred_element_type=F32)


def columns_kernel(x_ref, high_ref, low_ref, out_ref, x_high, x_low):
    @pl.when(pl.program_id(0) == 0)
    def _():
        x_high[...], x_low[...] = split(x_ref[...])

    high = high_ref[...]
    out_ref[...] = (
        mul(x_high[...], high) + mul(x_low[...], high) + mul(x_high[...], low_ref[...])
    )


def times_table(values, table):
    rows, depth = values.shape
    width = table[0].shape[1]
    block = min(256, width)
    return pl.pallas_call(
        columns_kernel,
        grid=(width // block,),
        out_shape=jax.ShapeDtypeStruct((rows, width), F32),
        in_specs=[
            pl.BlockSpec((rows, depth), lambda i: (0, 0)),
            pl.BlockSpec((depth, block), lambda i: (0, i)),
            pl.BlockSpec((depth, block), lambda i: (0, i)),
        ],
        out_specs=pl.BlockSpec((rows, block), lambda i: (0, i)),
        scratch_shapes=[pltpu.VMEM((rows, depth), BF16)] * 2,
    )(values, *table)


def rows_kernel(high_ref, low_ref, x_ref, out_ref, x_high, x_low):
    @pl.when(pl.program_id(0) == 0)
    def _():
        x_high[...], x_low[...] = split(x_ref[...])

    for n in range(x_ref.shape[0]):
        out_ref[n] = (
            mul(high_ref[...], x_high[n])
            + mul(high_ref[...], x_low[n])
            + mul(low_ref[...], x_high[n])
        )


def table_times(table, values):
    steps, depth, width = values.shape
    height = table[0].shape[0]
    block = min(256, height)
    return pl.pallas_call(
        rows_kernel,
        grid=(height // block,),
        out_shape=jax.ShapeDtypeStruct((steps, height, width), F32),
        in_specs=[
            pl.BlockSpec((block, depth), lambda i: (i, 0)),
            pl.BlockSpec((block, depth), lambda i: (i, 0)),
            pl.BlockSpec((steps, depth, width), lambda i: (0, 0, 0)),
        ],
        out_specs=pl.BlockSpec((steps, block, width), lambda i: (0, i, 0)),
        scratch_shapes=[pltpu.VMEM((steps, depth, width), BF16)] * 2,
    )(*table, values)


def power_kernel(choice_ref, table_ref, out_ref):
    steps, blocks, _, width = out_ref.shape
    across = width // TILE
    for n in range(steps):
        for b in range(blocks):
            for x in range(across):
                picked = choice_ref[n, b * across + x]
                out_ref[n, b, :, x * TILE : (x + 1) * TILE] = table_ref[picked]


def power_of(pattern_choice, tables, first_row, strip, width):
    steps = pattern_choice.shape[0]
    part = min(TILE, strip)
    blocks = strip // part
    offset = first_row % TILE if strip < TILE else 0
    tiles = lax.dynamic_slice_in_dim(tables, offset, part, axis=1)
    chosen = lax.dynamic_slice_in_dim(pattern_choice, first_row // TILE, blocks, axis=1)
    power = pl.pallas_call(
        power_kernel,
        out_shape=jax.ShapeDtypeStruct((steps, blocks, part, width), F32),
        in_specs=[
            pl.BlockSpec(memory_space=pltpu.SMEM),
            pl.BlockSpec(memory_space=pltpu.VMEM),
        ],
        out_specs=pl.BlockSpec(memory_space=pltpu.VMEM),
    )(chosen.reshape(steps, -1), tiles)
    return power.reshape(steps, strip, width)


def divergence(warmth, kappa, inner):
    def face(low, high):
        return 1.0 if kappa is None else 0.5 * (low + high)

    k = warmth if kappa is None else kappa
    upward = face(k[:, 1:], k[:, :-1]) * (warmth[:, 1:] - warmth[:, :-1])
    upward = jnp.where(inner[None, :, None], upward, 0.0)
    centre, k_mid = warmth[:, 1:-1], k[:, 1:-1]
    lateral = CROSS_WEIGHT * (
        face(k_mid[:, :, 1:], k_mid[:, :, :-1]) * (centre[:, :, 1:] - centre[:, :, :-1])
    )
    zero = jnp.zeros_like(centre[:, :, :1])
    across = jnp.concatenate([lateral, zero], 2) - jnp.concatenate([zero, lateral], 2)
    return upward[:, 1:] - upward[:, :-1] + across


def mode_factors(row_ids, column_ids, height, width, conduct):
    mu_rows = 2.0 - 2.0 * jnp.cos(row_ids.astype(F32) * (math.pi / height))
    mu_cols = 2.0 - 2.0 * jnp.cos(column_ids.astype(F32) * (math.pi / width))
    rate = conduct * (mu_rows[:, None] + CROSS_WEIGHT * mu_cols[None, :])
    gain = 1.0 / (1.0 / TIMESTEP_SIZE + rate)
    return gain, gain * (1.0 / TIMESTEP_SIZE)


def shards(
    initial_warmth,
    pattern_choice,
    dissipation_tables,
    material_label,
    intercept_kappa,
    sensitivity_coef,
):
    steps = pattern_choice.shape[0]
    strip, width = initial_warmth.shape
    tm_count = lax.axis_size("tm")
    rows_count = lax.axis_size("rows")
    height = strip * rows_count
    first_row = lax.axis_index("rows") * strip
    power = power_of(pattern_choice, dissipation_tables, first_row, strip, width)

    padded_rows = first_row - 1 + jnp.arange(strip + 2, dtype=jnp.int32)
    labels = jnp.take(material_label, jnp.clip(padded_rows, 0, height - 1) // TILE, axis=0)
    base_tiles = jnp.zeros(labels.shape, F32)
    slope_tiles = jnp.zeros(labels.shape, F32)
    for label in range(intercept_kappa.shape[0]):
        base_tiles = jnp.where(labels == label, intercept_kappa[label], base_tiles)
        slope_tiles = jnp.where(labels == label, sensitivity_coef[label], slope_tiles)
    base = jnp.repeat(base_tiles, TILE, axis=1)[None]
    slope = jnp.repeat(slope_tiles, TILE, axis=1)[None]
    upper_rows = padded_rows[:-1]
    inner = (upper_rows >= 0) & (upper_rows + 1 <= height - 1)
    conduct = jnp.mean(intercept_kappa)

    column_cos = cosine_table(width)
    row_cos = cosine_table(height)
    columns_out, columns_in = two_parts(column_cos.T), two_parts(column_cos)
    if height == width:
        rows_out, rows_in = columns_in, columns_out
    else:
        rows_out, rows_in = two_parts(row_cos), two_parts(row_cos.T)

    narrow = width // rows_count
    share = height // tm_count
    column_ids = lax.axis_index("rows") * narrow + jnp.arange(narrow, dtype=jnp.int32)
    all_rows = jnp.arange(height, dtype=jnp.int32)
    own_rows = lax.axis_index("tm") * share + jnp.arange(share, dtype=jnp.int32)
    gain, keep = mode_factors(all_rows, column_ids, height, width, conduct)
    weight = (jnp.where(all_rows == 0, 1.0, 2.0) / height)[:, None] * (
        jnp.where(column_ids == 0, 1.0, 2.0) / width
    )[None, :]
    _, own_keep = mode_factors(own_rows, column_ids, height, width, conduct)
    block_keep = own_keep
    for _ in range(steps - 1):
        block_keep = block_keep * own_keep
    around = block_keep
    for _ in range(tm_count - 1):
        around = around * block_keep
    closing = ALPHA / (1.0 - ALPHA * around)
    first_block = lax.axis_index("tm") == 0

    start = extended(initial_warmth[None], "rows", 1)
    start_div = divergence(start, base * (1.0 + slope * jnp.tanh(start)), inner)
    warmth = jnp.broadcast_to(initial_warmth[None], (steps, strip, width))
    wrapped = None
    for sweep in range(ITERS):
        if sweep == 0:
            resid = power + start_div
        else:
            grid = extended(warmth, "rows", 1)
            div = divergence(grid, base * (1.0 + slope * jnp.tanh(grid)), inner)
            resid = div - last_div - conduct * divergence(grid - last_grid, None, inner)
        modes = times_table(resid.reshape(steps * strip, width), columns_out)
        modes = lax.all_to_all(
            modes.reshape(steps, strip, width), "rows", split_axis=2, concat_axis=1, tiled=True
        )
        modes = table_times(rows_out, modes)
        sources = [modes[n] * weight for n in range(steps)]
        if wrapped is not None:
            sources[0] = sources[0] - jnp.where(first_block, wrapped / TIMESTEP_SIZE, 0.0)
        sources = [gain * source for source in sources]
        block_end = sources[0]
        for source in sources[1:]:
            block_end = source + keep * block_end
        ends = lax.all_to_all(block_end, "tm", split_axis=0, concat_axis=0, tiled=True)
        ends = ends.reshape(tm_count, share, narrow)
        last = ends[0]
        for k in range(1, tm_count):
            last = ends[k] + block_keep * last
        entry = [closing * last]
        for k in range(tm_count - 1):
            entry.append(ends[k] + block_keep * entry[k])
        entry = jnp.concatenate(entry, 0)
        carry = lax.all_to_all(entry, "tm", split_axis=0, concat_axis=0, tiled=True)
        wrapped = carry
        solved = []
        for source in sources:
            carry = source + keep * carry
            solved.append(carry)
        field = table_times(rows_in, jnp.stack(solved, 0))
        field = lax.all_to_all(field, "rows", split_axis=1, concat_axis=2, tiled=True)
        update = times_table(field.reshape(steps * strip, width), columns_in)
        if sweep == 0:
            last_grid, last_div = start, start_div
        else:
            last_grid, last_div = grid, div
        warmth = warmth + update.reshape(steps, strip, width)
    return warmth


def solution(mesh):
    in_specs = (P("rows", None), P("tm", None, None), P(), P(), P(), P())
    out_specs = P("tm", "rows", None)
    return jax.shard_map(shards, mesh=mesh, in_specs=in_specs, out_specs=out_specs, check_vma=False)
```

profile of v0, /device:TPU:1, one launch (start us, length us, event | category | flops | bytes accessed | tf_op | source)
XLA Modules:
  0.0 391.1 jit_solution(3354852746309055998)
XLA Ops:
  2.7 4.5 %collective-permute-start = (f32[1,1,1024]{2,1,0:T(1,128)S(1)}, f32[1,1,1024]{2,1,0:T(1,128)S(1)}, u32[]{:S(2)}, u32[]{:S(2)}) collective-permute-start(f32[1,1,1024]{2,1,0:T(1,128)S(1)} %get-tuple-element.36), channel_id=1, source_target_pairs={{0,1},{1,2},{2,3},{4,5},{5,6},{6,7},{8,9},{9,10},{10,11},{12,13},{... | collective-permute-start | bytes 12296 | tf_op jit(solution)/shard_map/ppermute | solution.py:24
  30.5 7.5 %shard_map.101 = f32[512,1024]{1,0:T(8,128)} custom-call(f32[512,1024]{1,0:T(8,128)} %bitcast_add_fusion.x_ref, bf16[1024,1024]{1,0:T(8,128)(2,1)} %constant.63.clone.high_ref, bf16[1024,1024]{1,0:T(8,128)(2,1)} %constant.64.clone.low_ref), custom_call_target="tpu_custom_call" | custom-call | tf_op jit(solution)/shard_map/pallas_call | solution.py:68
  38.0 4.1 %copy.19 = f32[2,256,1024]{1,0,2:T(2,128)} copy(f32[2,256,1024]{2,1,0:T(8,128)} %bitcast.243) | data formatting | bytes 4194304 | tf_op jit(solution)/shard_map/reshape | solution.py:235
  42.1 3.7 all-to-all-start
  47.2 21.6 %all-to-all-done = f32[2,256,1024]{1,0,2:T(2,128)S(1)} async-done(((f32[2,256,1024]{1,0,2:T(2,128)}), f32[2,256,1024]{1,0,2:T(2,128)S(1)}, u32[]{:S(2)}, u32[]{:S(2)}) %all-to-all-start) | async-done | bytes 2097184 | tf_op jit(solution)/shard_map/all_to_all | solution.py:234
  73.2 7.5 %shard_map.102 = f32[2,1024,256]{2,1,0:T(8,128)} custom-call(bf16[1024,1024]{1,0:T(8,128)(2,1)} %constant.65.clone.high_ref, bf16[1024,1024]{1,0:T(8,128)(2,1)} %constant.124.clone.low_ref, f32[2,1024,256]{2,1,0:T(8,128)} %bitcast.244), custom_call_target="tpu_custom_call" | custom-call | tf_op jit(solution)/shard_map/pallas_call | solution.py:99
  83.8 6.6 %all-to-all-start.1 = ((f32[8,128,256]{2,1,0:T(8,128)}), f32[8,128,256]{2,1,0:T(8,128)S(1)}, u32[]{:S(2)}, u32[]{:S(2)}) async-start(f32[8,128,256]{2,1,0:T(8,128)} %fusion.27), calls=%async_computation.1 | async-start | bytes 2097152 | tf_op jit(solution)/shard_map/all_to_all | solution.py:245
  90.5 24.6 %all-to-all-done.1 = f32[8,128,256]{2,1,0:T(8,128)S(1)} async-done(((f32[8,128,256]{2,1,0:T(8,128)}), f32[8,128,256]{2,1,0:T(8,128)S(1)}, u32[]{:S(2)}, u32[]{:S(2)}) %all-to-all-start.1) | async-done | bytes 1048608 | tf_op jit(solution)/shard_map/all_to_all | solution.py:245
  121.7 4.9 %all-to-all-start.2 = ((f32[8,128,256]{2,1,0:T(8,128)}), f32[8,128,256]{2,1,0:T(8,128)}, u32[]{:S(2)}, u32[]{:S(2)}) async-start(f32[8,128,256]{2,1,0:T(8,128)} %bitcast.257), calls=%async_computation.2 | async-start | bytes 2097152 | tf_op jit(solution)/shard_map/all_to_all | solution.py:254
  126.6 24.7 %all-to-all-done.2 = f32[8,128,256]{2,1,0:T(8,128)} async-done(((f32[8,128,256]{2,1,0:T(8,128)}), f32[8,128,256]{2,1,0:T(8,128)}, u32[]{:S(2)}, u32[]{:S(2)}) %all-to-all-start.2) | async-done | bytes 1048608 | tf_op jit(solution)/shard_map/all_to_all | solution.py:254
  154.6 7.5 %shard_map.103 = f32[2,1024,256]{2,1,0:T(8,128)} custom-call(bf16[1024,1024]{1,0:T(8,128)(2,1)} %constant.63.clone.high_ref, bf16[1024,1024]{1,0:T(8,128)(2,1)} %constant.64.clone.low_ref, f32[2,1024,256]{2,1,0:T(8,128)} %pad_maximum_fusion.1.x_ref), custom_call_target="tpu_custom_call" | custom-call | tf_op jit(solution)/shard_map/pallas_call | solution.py:99
  165.2 29.4 %all_to_all.102 = f32[2,1024,256]{2,0,1:T(2,128)S(1)} all-to-all(f32[2,1024,256]{2,0,1:T(2,128)S(1)} %copy.22), channel_id=1, replica_groups=mesh['tm'=8,'rows'=4] {'rows'}, dimensions={1} | all-to-all | bytes 4194304 | tf_op jit(solution)/shard_map/all_to_all | solution.py:261
  197.8 7.6 %shard_map.104 = f32[512,1024]{1,0:T(8,128)} custom-call(f32[512,1024]{1,0:T(8,128)} %bitcast.245, bf16[1024,1024]{1,0:T(8,128)(2,1)} %constant.65.clone.high_ref, bf16[1024,1024]{1,0:T(8,128)(2,1)} %constant.124.clone.low_ref), custom_call_target="tpu_custom_call" | custom-call | tf_op jit(solution)/shard_map/pallas_call | solution.py:68
  221.1 7.5 %shard_map.105 = f32[512,1024]{1,0:T(8,128)} custom-call(f32[512,1024]{1,0:T(8,128)} %bitcast.234, bf16[1024,1024]{1,0:T(8,128)(2,1)} %constant.63.clone.high_ref, bf16[1024,1024]{1,0:T(8,128)(2,1)} %constant.64.clone.low_ref), custom_call_target="tpu_custom_call" | custom-call | tf_op jit(solution)/shard_map/pallas_call | solution.py:68
  228.7 4.1 %copy.24 = f32[2,256,1024]{1,0,2:T(2,128)} copy(f32[2,256,1024]{2,1,0:T(8,128)} %bitcast.246) | data formatting | bytes 4194304 | tf_op jit(solution)/shard_map/reshape | solution.py:235
  232.8 3.6 all-to-all-start.4
  236.4 24.2 %all-to-all-done.4 = f32[2,256,1024]{1,0,2:T(2,128)S(1)} async-done(((f32[2,256,1024]{1,0,2:T(2,128)}), f32[2,256,1024]{1,0,2:T(2,128)S(1)}, u32[]{:S(2)}, u32[]{:S(2)}) %all-to-all-start.4) | async-done | bytes 2097184 | tf_op jit(solution)/shard_map/all_to_all | solution.py:234
  265.0 7.5 %shard_map.106 = f32[2,1024,256]{2,1,0:T(8,128)} custom-call(bf16[1024,1024]{1,0:T(8,128)(2,1)} %constant.65.clone.high_ref, bf16[1024,1024]{1,0:T(8,128)(2,1)} %constant.124.clone.low_ref, f32[2,1024,256]{2,1,0:T(8,128)} %bitcast.247), custom_call_target="tpu_custom_call" | custom-call | tf_op jit(solution)/shard_map/pallas_call | solution.py:99
  276.0 27.7 %all_to_all.103 = f32[8,128,256]{2,1,0:T(8,128)S(1)} all-to-all(f32[8,128,256]{2,1,0:T(8,128)S(1)} %fusion.31), channel_id=1, replica_groups=mesh['tm'=8,'rows'=4] {'tm'}, dimensions={0} | all-to-all | bytes 2097152 | tf_op jit(solution)/shard_map/all_to_all | solution.py:245
  304.8 29.0 %all_to_all.104 = f32[8,128,256]{2,1,0:T(8,128)S(1)} all-to-all(f32[8,128,256]{2,1,0:T(8,128)S(1)} %bitcast.258), channel_id=1, replica_groups=mesh['tm'=8,'rows'=4] {'tm'}, dimensions={0} | all-to-all | bytes 2097152 | tf_op jit(solution)/shard_map/all_to_all | solution.py:254
  337.1 7.4 %shard_map.107 = f32[2,1024,256]{2,1,0:T(8,128)} custom-call(bf16[1024,1024]{1,0:T(8,128)(2,1)} %constant.63.clone.high_ref, bf16[1024,1024]{1,0:T(8,128)(2,1)} %constant.64.clone.low_ref, f32[2,1024,256]{2,1,0:T(8,128)} %pad_maximum_fusion.2.x_ref), custom_call_target="tpu_custom_call" | custom-call | tf_op jit(solution)/shard_map/pallas_call | solution.py:99
  347.7 29.0 %all_to_all.105 = f32[2,1024,256]{2,0,1:T(2,128)S(1)} all-to-all(f32[2,1024,256]{2,0,1:T(2,128)S(1)} %copy.27), channel_id=1, replica_groups=mesh['tm'=8,'rows'=4] {'rows'}, dimensions={1} | all-to-all | bytes 4194304 | tf_op jit(solution)/shard_map/all_to_all | solution.py:261
  379.9 7.7 %shard_map.108 = f32[512,1024]{1,0:T(8,128)} custom-call(f32[512,1024]{1,0:T(8,128)} %bitcast.242, bf16[1024,1024]{1,0:T(8,128)(2,1)} %constant.65.clone.high_ref, bf16[1024,1024]{1,0:T(8,128)(2,1)} %constant.124.clone.low_ref), custom_call_target="tpu_custom_call" | custom-call | tf_op jit(solution)/shard_map/pallas_call | solution.py:68
  387.6 3.5 fusion.65
  (114 shorter events, 84.4 us)
Async XLA Ops:
  0.0 17.2 %copy-start = (s32[2,8,8]{2,1,0:T(8,128)S(1)}, s32[2,8,8]{2,1,0:T(8,128)}, u32[]{:S(2)}) copy-start(s32[2,8,8]{2,1,0:T(8,128)} %param.11) | copy-start | bytes 1540
  0.8 22.5 %collective-permute-start.1 = (f32[1,1,1024]{2,1,0:T(1,128)S(1)}, f32[1,1,1024]{2,1,0:T(1,128)S(1)}, u32[]{:S(2)}, u32[]{:S(2)}) collective-permute-start(f32[1,1,1024]{2,1,0:T(1,128)S(1)} %get-tuple-element.37), channel_id=1, source_target_pairs={{1,0},{2,1},{3,2},{5,4},{6,5},{7,6},{9,8},{10,9},{11,10},{13,12},{... | collective-permute-start | bytes 12296 | tf_op jit(solution)/shard_map/ppermute | solution.py:27
  2.7 20.6 %collective-permute-start = (f32[1,1,1024]{2,1,0:T(1,128)S(1)}, f32[1,1,1024]{2,1,0:T(1,128)S(1)}, u32[]{:S(2)}, u32[]{:S(2)}) collective-permute-start(f32[1,1,1024]{2,1,0:T(1,128)S(1)} %get-tuple-element.36), channel_id=1, source_target_pairs={{0,1},{1,2},{2,3},{4,5},{5,6},{6,7},{8,9},{9,10},{10,11},{12,13},{... | collective-permute-start | bytes 12296 | tf_op jit(solution)/shard_map/ppermute | solution.py:24
  18.2 1.0 copy-start.7
  19.5 3.8 copy-start.9
  19.5 3.8 copy-start.2
  26.9 2.0 copy-start.13
  42.1 3.7 copy-start.16
  42.1 26.7 %all-to-all-start = ((f32[2,256,1024]{1,0,2:T(2,128)}), f32[2,256,1024]{1,0,2:T(2,128)S(1)}, u32[]{:S(2)}, u32[]{:S(2)}) async-start(f32[2,256,1024]{1,0,2:T(2,128)} %copy.19), calls=%async_computation | async-start | bytes 4194304 | tf_op jit(solution)/shard_map/all_to_all | solution.py:234
  83.8 31.2 %all-to-all-start.1 = ((f32[8,128,256]{2,1,0:T(8,128)}), f32[8,128,256]{2,1,0:T(8,128)S(1)}, u32[]{:S(2)}, u32[]{:S(2)}) async-start(f32[8,128,256]{2,1,0:T(8,128)} %fusion.27), calls=%async_computation.1 | async-start | bytes 2097152 | tf_op jit(solution)/shard_map/all_to_all | solution.py:245
  115.1 1.0 copy-start.6
  116.2 35.1 %copy-start.5 = (f32[2,1024,256]{2,1,0:T(8,128)S(1)}, f32[2,1024,256]{2,1,0:T(8,128)}, u32[]{:S(2)}) copy-start(f32[2,1024,256]{2,1,0:T(8,128)} %shard_map.102) | copy-start | bytes 6291460
  120.7 1.0 copy-start.15
  121.7 29.6 %all-to-all-start.2 = ((f32[8,128,256]{2,1,0:T(8,128)}), f32[8,128,256]{2,1,0:T(8,128)}, u32[]{:S(2)}, u32[]{:S(2)}) async-start(f32[8,128,256]{2,1,0:T(8,128)} %bitcast.257), calls=%async_computation.2 | async-start | bytes 2097152 | tf_op jit(solution)/shard_map/all_to_all | solution.py:254
  205.4 7.7 %copy-start.10 = (f32[258,8,128]{2,1,0:T(8,128)S(1)}, f32[258,8,128]{2,1,0:T(8,128)}, u32[]{:S(2)}) copy-start(f32[258,8,128]{2,1,0:T(8,128)} %copy-done.9) | copy-start | bytes 3170308
  207.3 5.8 %copy-start.8 = (f32[258,8,128]{2,1,0:T(8,128)S(1)}, f32[258,8,128]{2,1,0:T(8,128)}, u32[]{:S(2)}) copy-start(f32[258,8,128]{2,1,0:T(8,128)} %copy-done.7) | copy-start | bytes 3170308
  207.4 6.3 %collective-permute-start.3 = (f32[2,1,1024]{2,1,0:T(1,128)S(1)}, f32[2,1,1024]{2,1,0:T(1,128)S(1)}, u32[]{:S(2)}, u32[]{:S(2)}) collective-permute-start(f32[2,1,1024]{2,1,0:T(1,128)S(1)} %get-tuple-element.31), channel_id=1, source_target_pairs={{1,0},{2,1},{3,2},{5,4},{6,5},{7,6},{9,8},{10,9},{11,10},{13,12},{... | collective-permute-start | bytes 24584 | tf_op jit(solution)/shard_map/ppermute | solution.py:27
  210.5 3.4 collective-permute-start.2
  213.3 1.2 copy-start.14
  217.2 1.2 copy-start.12
  232.8 27.9 %all-to-all-start.4 = ((f32[2,256,1024]{1,0,2:T(2,128)}), f32[2,256,1024]{1,0,2:T(2,128)S(1)}, u32[]{:S(2)}, u32[]{:S(2)}) async-start(f32[2,256,1024]{1,0,2:T(2,128)} %copy.24), calls=%async_computation.4 | async-start | bytes 4194304 | tf_op jit(solution)/shard_map/all_to_all | solution.py:234
  304.3 29.5 %copy-start.4 = (f32[2,1024,256]{2,1,0:T(8,128)S(1)}, f32[2,1024,256]{2,1,0:T(8,128)}, u32[]{:S(2)}) copy-start(f32[2,1024,256]{2,1,0:T(8,128)} %shard_map.106) | copy-start | bytes 6291460
  379.9 7.7 %copy-start.3 = (f32[512,1024]{1,0:T(8,128)S(1)}, f32[512,1024]{1,0:T(8,128)}, u32[]{:S(2)}) copy-start(f32[512,1024]{1,0:T(8,128)} %shard_map.104) | copy-start | bytes 6291460
  387.6 3.5 copy-start.1
  (1 other events, 1.0 us)
where the time goes:
time: 394 us; the launch traced here: 391 us
  blocking collectives  115 us (29%)
  waiting for transfers between devices  95.2 us (24%)
  Pallas kernels  62.7 us (16%)
  local copies, waits for them, and re-layouts  46.5 us (12%)
  other arithmetic  39.4 us (10%)
  starting transfers between devices  31 us (8%)
    all_to_all x2, blocking collectives, shards(): lax.all_to_all(field, 'rows', split_axis=1, concat_axis=2, tiled=True)  58.4 us
    all_to_all x2, waiting for transfers between devices, shards(): lax.all_to_all(modes.reshape(steps, strip, width), 'rows', split_axis=2,...  45.9 us
    pallas_call x4, Pallas kernels, times_table(): pl.pallas_call(columns_kernel, grid=(width // block,), out_shape=jax.Shap...  30.3 us
    pallas_call x4, Pallas kernels, table_times(): pl.pallas_call(rows_kernel, grid=(height // block,), out_shape=jax.ShapeD...  29.8 us
    all_to_all x1, blocking collectives, shards(): carry = lax.all_to_all(entry, 'tm', split_axis=0, concat_axis=0, tiled=True)  29 us
    all_to_all x1, blocking collectives, shards(): lax.all_to_all(block_end, 'tm', split_axis=0, concat_axis=0, tiled=True)  27.7 us
    all_to_all x1, waiting for transfers between devices, shards(): carry = lax.all_to_all(entry, 'tm', split_axis=0, concat_axis=0, tiled=True)  24.7 us
    all_to_all x1, waiting for transfers between devices, shards(): lax.all_to_all(block_end, 'tm', split_axis=0, concat_axis=0, tiled=True)  24.6 us
  transfers between devices with their start and end apart: 8, of which 5 were waited for; matrix products, arithmetic and copies ran while one was open for 4% of the time, Pallas kernels for 1%

commit v1 on v0

--- a/solution.py
+++ b/solution.py
@@ -1,4 +1,5 @@
 import math
+from types import SimpleNamespace
 
 import jax
 import jax.numpy as jnp
@@ -268,7 +269,836 @@
     return warmth
 
 
+LANES = 128
+EDGE = 8
+ROWS = 32
+MESH = pl.DeviceIdType.MESH
+
+
+def dot3(left_high, left_low, right_high, right_low):
+    return mul(left_high, right_high) + mul(left_low, right_high) + mul(left_high, right_low)
+
+
+def remote(src, dst, send_sem, recv_sem, device):
+    return pltpu.make_async_remote_copy(
+        src_ref=src,
+        dst_ref=dst,
+        send_sem=send_sem,
+        recv_sem=recv_sem,
+        device_id=device,
+        device_id_type=MESH,
+    )
+
+
+def scratch_of(steps, strip, length, tm_count, rows_count):
+    narrow = length // rows_count
+    chunks = narrow // LANES
+    half = length // 2
+    units = half // LANES
+    wide = steps * LANES
+    padded = strip + 2 * EDGE
+    peers = rows_count - 1
+
+    def f32(*shape):
+        return pltpu.VMEM(shape, F32)
+
+    def b16(*shape):
+        return pltpu.VMEM(shape, BF16)
+
+    dma = pltpu.SemaphoreType.DMA
+    return dict(
+        ch=b16(length, length),
+        cl=b16(length, length),
+        cth=b16(length, length),
+        ctl=b16(length, length),
+        ph=b16(length, length),
+        pl=b16(length, length),
+        th=b16(8, TILE, TILE),
+        tl=b16(8, TILE, TILE),
+        base=f32(8, length),
+        slope=f32(8, length),
+        w0p=f32(padded, length),
+        kp=f32(padded, length),
+        div0=f32(strip, length),
+        halo=f32(2, EDGE, length),
+        dst=f32(peers, strip, narrow),
+        xd=f32(length, narrow),
+        xh=b16(chunks, length, wide),
+        xl=b16(chunks, length, wide),
+        fx=f32(chunks, rows_count, strip, wide),
+        xr=f32(chunks, length, wide),
+        ss=f32(chunks, length, wide),
+        e=f32(ITERS, chunks, length, LANES),
+        er=f32(ITERS, chunks, half, LANES),
+        fin=f32(ITERS, chunks, half, LANES),
+        sin=f32(ITERS, chunks, half, LANES),
+        fout=f32(ITERS, chunks, half, LANES),
+        sout=f32(ITERS, chunks, half, LANES),
+        cs=f32(ITERS, chunks, half, LANES),
+        zz=f32(half, LANES),
+        carry=f32(ITERS, chunks, length, LANES),
+        ctot=f32(chunks, length, LANES),
+        gw=f32(chunks, length, LANES),
+        keep=f32(chunks, length, LANES),
+        rho=f32(chunks, length, LANES),
+        sd=f32(chunks, length, LANES),
+        k1=f32(chunks, half, LANES),
+        k2=f32(chunks, half, LANES),
+        pa=f32(chunks, half, LANES),
+        pb=f32(chunks, half, LANES),
+        pf=f32(chunks, half, LANES),
+        iy=f32(ITERS, chunks, length + 2 * EDGE, wide),
+        yr=f32(ITERS, chunks, rows_count, padded, wide),
+        uh=b16(length, wide),
+        ul=b16(length, wide),
+        lh=b16(steps * padded, rows_count * LANES),
+        ll=b16(steps * padded, rows_count * LANES),
+        u1p=f32(steps * padded, length),
+        tsem=dma((4,)),
+        hs=dma((2,)),
+        hr=dma((2,)),
+        ds=dma((peers,)),
+        dr=dma((peers,)),
+        xs=dma((chunks * peers,)),
+        xrs=dma((chunks * peers,)),
+        ys=dma((ITERS * chunks * peers,)),
+        yrs=dma((ITERS * chunks * peers,)),
+        es=dma((ITERS * chunks * units,)),
+        ers=dma((ITERS * chunks * units,)),
+        fs=dma((ITERS * chunks * units,)),
+        frs=dma((ITERS * chunks * units,)),
+        gs=dma((ITERS * chunks * units,)),
+        grs=dma((ITERS * chunks * units,)),
+        cts=dma((ITERS * chunks * units,)),
+        crs=dma((ITERS * chunks * units,)),
+    )
+
+
+INPUTS = [
+    "w0",
+    "choice",
+    "tables",
+    "label",
+    "icpt",
+    "sens",
+    "mup",
+    "muq",
+    "chh",
+    "clh",
+    "cthh",
+    "ctlh",
+]
+
+
+def fused_kernel(steps, strip, length, tm_count, rows_count, names, *refs):
+    s = SimpleNamespace(**dict(zip(names, refs)))
+    narrow = length // rows_count
+    chunks = narrow // LANES
+    half = length // 2
+    units = half // LANES
+    padded = strip + 2 * EDGE
+    blocks = strip // TILE
+    tiles = length // TILE
+    big = 2 * LANES
+    zs, ys_count = tm_count // 2, rows_count // 2
+
+    t, r = lax.axis_index("tm"), lax.axis_index("rows")
+    z, x = lax.div(t, 2), lax.rem(t, 2)
+    y, c = lax.div(r, 2), lax.rem(r, 2)
+    pair = t + 1 - 2 * x
+    peers = [(dy, dc) for dy in range(1, ys_count) for dc in range(2)] + [(0, 1)]
+
+    def to(dy, dc):
+        return lax.rem(y + dy, ys_count) * 2 + lax.rem(c + dc, 2)
+
+    def frm(dy, dc):
+        return lax.rem(y + ys_count - dy, ys_count) * 2 + lax.rem(c + 2 - dc, 2)
+
+    def rows_at(start, size):
+        return pl.ds(pl.multiple_of(start, size), size)
+
+    tables_in = [
+        pltpu.make_async_copy(a, b, s.tsem.at[i])
+        for i, (a, b) in enumerate(
+            [(s.cthh, s.cth), (s.ctlh, s.ctl), (s.chh, s.ch), (s.clh, s.cl)]
+        )
+    ]
+    for copy in tables_in:
+        copy.start()
+
+    barrier = pltpu.get_barrier_semaphore()
+    for dy, dc in peers:
+        pl.semaphore_signal(barrier, inc=1, device_id=(t, to(dy, dc)), device_id_type=MESH)
+    pl.semaphore_signal(barrier, inc=1, device_id=(pair, r), device_id_type=MESH)
+
+    @pl.when(z > 0)
+    def _():
+        pl.semaphore_signal(barrier, inc=1, device_id=(t - 2, r), device_id_type=MESH)
+
+    @pl.when(z < zs - 1)
+    def _():
+        pl.semaphore_signal(barrier, inc=1, device_id=(t + 2, r), device_id_type=MESH)
+
+    beside = lax.min(z, 1) + lax.min(zs - 1 - z, 1)
+    pl.semaphore_wait(barrier, len(peers) + 1 + beside)
+
+    def halo_down(to_row):
+        return remote(
+            s.w0.at[pl.ds(strip - EDGE, EDGE)], s.halo.at[0], s.hs.at[0], s.hr.at[0], (t, to_row)
+        )
+
+    def halo_up(to_row):
+        return remote(s.w0.at[pl.ds(0, EDGE)], s.halo.at[1], s.hs.at[1], s.hr.at[1], (t, to_row))
+
+    @pl.when(r < rows_count - 1)
+    def _():
+        halo_down(r + 1).start()
+
+    @pl.when(r > 0)
+    def _():
+        halo_up(r - 1).start()
+
+    count = s.icpt.shape[0]
+    total = s.icpt[0]
+    for i in range(1, count):
+        total = total + s.icpt[i]
+    conduct = total / count
+    for i in range(blocks + 2):
+        ty = lax.min(lax.max(r * blocks - 1 + i, 0), tiles - 1)
+        for tx in range(tiles):
+            label = s.label[ty, tx]
+            s.base[i : i + 1, tx * TILE : (tx + 1) * TILE] = jnp.full((1, TILE), s.icpt[label], F32)
+            s.slope[i : i + 1, tx * TILE : (tx + 1) * TILE] = jnp.full((1, TILE), s.sens[label], F32)
+
+    for j in range(chunks):
+
+        def factors(i, _, j=j):
+            rows = rows_at(i * LANES, LANES)
+            rate = conduct * (s.mup[rows] + CROSS_WEIGHT * s.muq[r * chunks + j, 0:1, :])
+            gain = 1.0 / (1.0 / TIMESTEP_SIZE + rate)
+            keep = gain * (1.0 / TIMESTEP_SIZE)
+            p = i * LANES + lax.broadcasted_iota(jnp.int32, (LANES, LANES), 0)
+            q = r * narrow + j * LANES + lax.broadcasted_iota(jnp.int32, (LANES, LANES), 1)
+            weight = (jnp.where(p == 0, 1.0, 2.0) / length) * (jnp.where(q == 0, 1.0, 2.0) / length)
+            s.gw[j, rows] = gain * weight
+            s.keep[j, rows] = keep
+            one = 1.0 + keep
+            k = keep * keep
+            around, power = one, k
+            for _ in range(tm_count - 1):
+                around = one + k * around
+                power = power * k
+            first = ALPHA * around / (1.0 - ALPHA * power)
+            s.rho[j, rows] = lax.fori_loop(0, t, lambda _, a: one + k * a, first)
+            return 0
+
+        lax.fori_loop(0, length // LANES, factors, 0)
+
+        def chain(i, _, j=j):
+            rows = rows_at(i * LANES, LANES)
+            keep = s.keep[j, rows_at(x * half + i * LANES, LANES)]
+            k = keep * keep
+            k2 = k * k
+            ones = jnp.ones_like(k)
+            whole = k2
+            for _ in range(zs - 1):
+                whole = whole * k2
+            upper = lax.fori_loop(0, zs - 1 - z, lambda _, a: a * k2, ones)
+            lower = lax.fori_loop(0, z, lambda _, a: a * k2, ones)
+            close = lower * (ALPHA / (1.0 - ALPHA * whole))
+            s.k1[j, rows] = k
+            s.k2[j, rows] = k2
+            s.pa[j, rows] = upper
+            s.pb[j, rows] = close
+            s.pf[j, rows] = 1.0 + close * (upper * k2)
+            return 0
+
+        lax.fori_loop(0, units, chain, 0)
+
+    @pl.when(z == 0)
+    def _():
+        s.fin[...] = jnp.zeros_like(s.fin)
+
+    @pl.when(z == zs - 1)
+    def _():
+        s.sin[...] = jnp.zeros_like(s.sin)
+
+    for j in range(chunks):
+        s.iy[0, j, 0:EDGE] = jnp.zeros((EDGE, steps * LANES), F32)
+        s.iy[0, j, length + EDGE :] = jnp.zeros((EDGE, steps * LANES), F32)
+    for k in range(s.tables.shape[0]):
+        s.th[k], s.tl[k] = split(s.tables[k])
+
+    s.w0p[EDGE : EDGE + strip] = s.w0[...]
+
+    @pl.when(r > 0)
+    def _():
+        halo_down(r).wait_recv()
+        s.w0p[0:EDGE] = s.halo[0]
+
+    @pl.when(r == 0)
+    def _():
+        s.w0p[0:EDGE] = jnp.broadcast_to(s.w0[0:1], (EDGE, length))
+
+    @pl.when(r < rows_count - 1)
+    def _():
+        halo_up(r).wait_recv()
+        s.w0p[EDGE + strip :] = s.halo[1]
+
+    @pl.when(r == rows_count - 1)
+    def _():
+        s.w0p[EDGE + strip :] = jnp.broadcast_to(s.w0[strip - 1 :], (EDGE, length))
+
+    def kappa(offset):
+        def part(start, size, i):
+            rows = pl.ds(start, size)
+            warmth = s.w0p[rows]
+            if offset is not None:
+                warmth = warmth + s.u1p[pl.ds(offset + start, size)]
+            bent = s.slope[i : i + 1] * jnp.tanh(warmth)
+            s.kp[rows] = s.base[i : i + 1] * (1.0 + bent)
+
+        part(0, EDGE, 0)
+        part(EDGE + strip, EDGE, blocks + 1)
+        for b in range(blocks):
+
+            def inner(i, _, b=b):
+                part(pl.multiple_of(EDGE + b * TILE + i * ROWS, EDGE), ROWS, b + 1)
+                return 0
+
+            lax.fori_loop(0, TILE // ROWS, inner, 0)
+
+    lane = lax.broadcasted_iota(jnp.int32, (ROWS, length), 1)
+    ext = ROWS + 2 * EDGE
+
+    def forcing(offset, out_row):
+        def inner(i, _):
+            rows = pl.ds(pl.multiple_of(i * ROWS, ROWS), ext)
+            warmth, k = s.w0p[rows], s.kp[rows]
+            mid = slice(EDGE, EDGE + ROWS)
+            if offset is not None:
+                u = s.u1p[pl.ds(pl.multiple_of(offset + i * ROWS, EDGE), ext)]
+                warmth = warmth + u
+
+            def flux(shift, w, k, u):
+                value = 0.5 * (k + shift(k)) * (shift(w) - w)
+                if u is not None:
+                    value = value - conduct * (shift(u) - u)
+                return value
+
+            u = u if offset is not None else None
+            down = flux(lambda v: pltpu.roll(v, ext - 1, 0), warmth, k, u)
+            total = (down - pltpu.roll(down, 1, 0))[mid]
+            right = flux(
+                lambda v: pltpu.roll(v, length - 1, 1),
+                warmth[mid],
+                k[mid],
+                None if u is None else u[mid],
+            )
+            right = jnp.where(lane < length - 1, right, 0.0)
+            total = total + CROSS_WEIGHT * (right - pltpu.roll(right, 1, 1))
+            home = pl.ds(pl.multiple_of(i * ROWS, ROWS), ROWS)
+            if offset is None:
+                s.div0[home] = total
+            else:
+                total = total - s.div0[home]
+            rows = pl.ds(pl.multiple_of(out_row + i * ROWS, ROWS), ROWS)
+            s.ph[rows], s.pl[rows] = split(total)
+            return 0
+
+        lax.fori_loop(0, strip // ROWS, inner, 0)
+
+    kappa(None)
+    forcing(None, 0)
+
+    tables_in[0].wait()
+    tables_in[1].wait()
+
+    def send_d(k):
+        return remote(
+            s.dst.at[k],
+            s.xd.at[rows_at(r * strip, strip)],
+            s.ds.at[k],
+            s.dr.at[k],
+            (t, to(*peers[k])),
+        )
+
+    for k, peer in enumerate(peers + [(0, 0)]):
+        columns = rows_at(to(*peer) * narrow, narrow)
+        out = dot3(s.ph[0:strip], s.pl[0:strip], s.cth[:, columns], s.ctl[:, columns])
+        if k < len(peers):
+            s.dst[k] = out
+            send_d(k).start()
+        else:
+            s.xd[rows_at(r * strip, strip)] = out
+
+    own = rows_at(r * narrow, narrow)
+    for n in range(steps):
+
+        def place(ty, _, n=n):
+            rows = rows_at(ty * TILE, TILE)
+            for tx in range(tiles):
+                picked = s.choice[n, ty, tx]
+                s.ph[rows, tx * TILE : (tx + 1) * TILE] = s.th[picked]
+                s.pl[rows, tx * TILE : (tx + 1) * TILE] = s.tl[picked]
+            return 0
+
+        lax.fori_loop(0, tiles, place, 0)
+
+        def across(i, _, n=n):
+            rows = rows_at(i * half, half)
+            out = dot3(s.ph[rows], s.pl[rows], s.cth[:, own], s.ctl[:, own])
+            high, low = split(out)
+            for j in range(chunks):
+                s.xh[j, rows, n * LANES : (n + 1) * LANES] = high[:, j * LANES : (j + 1) * LANES]
+                s.xl[j, rows, n * LANES : (n + 1) * LANES] = low[:, j * LANES : (j + 1) * LANES]
+            return 0
+
+        lax.fori_loop(0, 2, across, 0)
+    tables_in[2].wait()
+    tables_in[3].wait()
+
+    def unit(sweep, j, i):
+        return (sweep * chunks + j) * units + i
+
+    def send_e(sweep, j, i):
+        n = unit(sweep, j, i)
+        return remote(
+            s.e.at[sweep, j, rows_at((1 - x) * half + i * LANES, LANES)],
+            s.er.at[sweep, j, rows_at(i * LANES, LANES)],
+            s.es.at[n],
+            s.ers.at[n],
+            (pair, r),
+        )
+
+    def send_f(sweep, j, i, device):
+        n = unit(sweep, j, i)
+        rows = rows_at(i * LANES, LANES)
+        return remote(
+            s.fout.at[sweep, j, rows], s.fin.at[sweep, j, rows], s.fs.at[n], s.frs.at[n], device
+        )
+
+    def send_s(sweep, j, i, device):
+        n = unit(sweep, j, i)
+        rows = rows_at(i * LANES, LANES)
+        return remote(
+            s.sout.at[sweep, j, rows], s.sin.at[sweep, j, rows], s.gs.at[n], s.grs.at[n], device
+        )
+
+    def send_c(sweep, j, i):
+        n = unit(sweep, j, i)
+        return remote(
+            s.cs.at[sweep, j, rows_at(i * LANES, LANES)],
+            s.carry.at[sweep, j, rows_at(x * half + i * LANES, LANES)],
+            s.cts.at[n],
+            s.crs.at[n],
+            (pair, r),
+        )
+
+    is_first = jnp.where(t == 0, 1.0, 0.0)
+
+    def rows_out(sweep, j):
+        per = big // LANES
+        parts = length // big
+
+        def block(i, _):
+            b = lax.rem(i + (1 - x) * (parts // 2), parts)
+            rows = rows_at(b * big, big)
+            out = dot3(s.ch[rows], s.cl[rows], s.xh[j], s.xl[j])
+            gw, keep = s.gw[j, rows], s.keep[j, rows]
+            first, second = out[:, :LANES] * gw, out[:, LANES:] * gw
+            if sweep > 0:
+                first = first - is_first * keep * s.ctot[j, rows]
+            s.ss[j, rows, :LANES] = first
+            s.ss[j, rows, LANES:] = second
+            s.e[sweep, j, rows] = second + keep * first
+
+            @pl.when(i < parts // 2)
+            def _():
+                for n in range(per):
+                    send_e(sweep, j, i * per + n).start()
+
+            return 0
+
+        lax.fori_loop(0, parts, block, 0)
+
+    def carries(sweep, j):
+        def halves(i):
+            mine = s.e[sweep, j, rows_at(x * half + i * LANES, LANES)]
+            other = s.er[sweep, j, rows_at(i * LANES, LANES)]
+            return jnp.where(x == 0, mine, other), jnp.where(x == 0, other, mine)
+
+        def pairs(i, _):
+            rows = rows_at(i * LANES, LANES)
+            send_e(sweep, j, i).wait_recv()
+            even, odd = halves(i)
+            block = odd + s.k1[j, rows] * even
+            s.zz[rows] = block
+
+            @pl.when(z == 0)
+            def _():
+                s.fout[sweep, j, rows] = block
+                send_f(sweep, j, i, (t + 2, r)).start()
+
+            @pl.when(z == zs - 1)
+            def _():
+                s.sout[sweep, j, rows] = block
+                send_s(sweep, j, i, (t - 2, r)).start()
+
+            return 0
+
+        lax.fori_loop(0, units, pairs, 0)
+
+        def relay_f(i):
+            rows = rows_at(i * LANES, LANES)
+
+            @pl.when(z > 0)
+            def _():
+                send_f(sweep, j, i, (t, r)).wait_recv()
+
+                @pl.when(z < zs - 1)
+                def _():
+                    s.fout[sweep, j, rows] = s.zz[rows] + s.k2[j, rows] * s.fin[sweep, j, rows]
+                    send_f(sweep, j, i, (t + 2, r)).start()
+
+        def relay_s(i):
+            rows = rows_at(i * LANES, LANES)
+
+            @pl.when(z < zs - 1)
+            def _():
+                send_s(sweep, j, i, (t, r)).wait_recv()
+                s.sout[sweep, j, rows] = s.sin[sweep, j, rows] + s.pa[j, rows] * s.zz[rows]
+
+                @pl.when(z > 0)
+                def _():
+                    send_s(sweep, j, i, (t - 2, r)).start()
+
+        def finish(i):
+            rows = rows_at(i * LANES, LANES)
+            even, _ = halves(i)
+            lower = s.fin[sweep, j, rows] * s.pf[j, rows] + s.pb[j, rows] * s.sout[sweep, j, rows]
+            upper = even + s.k1[j, rows] * lower
+            s.carry[sweep, j, rows_at(x * half + i * LANES, LANES)] = jnp.where(
+                x == 0, lower, upper
+            )
+            s.cs[sweep, j, rows] = jnp.where(x == 0, upper, lower)
+            send_c(sweep, j, i).start()
+
+        def run(first, second):
+            def one(i, _):
+                first(i)
+                return 0
+
+            def two(i, _):
+                second(i)
+                finish(i)
+                return 0
+
+            lax.fori_loop(0, units, one, 0)
+            lax.fori_loop(0, units, two, 0)
+
+        @pl.when(z < zs // 2)
+        def _():
+            run(relay_f, relay_s)
+
+        @pl.when(z >= zs // 2)
+        def _():
+            run(relay_s, relay_f)
+
+    def send_y(sweep, j, k):
+        n = (sweep * chunks + j) * len(peers) + k
+        target = to(*peers[k])
+        size = padded if sweep == 0 else strip
+        start = target * strip if sweep == 0 else target * strip + EDGE
+        return remote(
+            s.iy.at[sweep, j, pl.ds(pl.multiple_of(start, EDGE), size)],
+            s.yr.at[sweep, j, r, pl.ds(0, size)],
+            s.ys.at[n],
+            s.yrs.at[n],
+            (t, target),
+        )
+
+    def rows_in(sweep, j):
+        def wait(i, _):
+            send_c(sweep, j, i).wait_recv()
+            return 0
+
+        lax.fori_loop(0, units, wait, 0)
+
+        def solve(i, _):
+            rows = rows_at(i * LANES, LANES)
+            keep, carry = s.keep[j, rows], s.carry[sweep, j, rows]
+            first, second = s.ss[j, rows, :LANES], s.ss[j, rows, LANES:]
+            if sweep == 0:
+                steady = s.sd[j, rows]
+                first, second = first + steady, second + steady
+                carry = carry + s.rho[j, rows] * steady
+                s.ctot[j, rows] = carry
+            first = first + keep * carry
+            second = second + keep * first
+            s.uh[rows, :LANES], s.ul[rows, :LANES] = split(first)
+            s.uh[rows, LANES:], s.ul[rows, LANES:] = split(second)
+            return 0
+
+        lax.fori_loop(0, length // LANES, solve, 0)
+
+        def block(target):
+            rows = rows_at(target * strip, strip)
+            out = dot3(s.cth[rows], s.ctl[rows], s.uh[...], s.ul[...])
+            s.iy[sweep, j, pl.ds(pl.multiple_of(target * strip + EDGE, EDGE), strip)] = out
+
+        if sweep == 0:
+
+            def body(i, _):
+                block(i)
+                return 0
+
+            lax.fori_loop(0, rows_count, body, 0)
+            for k in range(len(peers)):
+                send_y(sweep, j, k).start()
+            s.yr[sweep, j, r] = s.iy[sweep, j, pl.ds(pl.multiple_of(r * strip, EDGE), padded)]
+        else:
+            for k, peer in enumerate(peers):
+                block(to(*peer))
+                send_y(sweep, j, k).start()
+            block(r)
+            mid = pl.ds(pl.multiple_of(r * strip + EDGE, EDGE), strip)
+            s.yr[sweep, j, r, 0:strip] = s.iy[sweep, j, mid]
+
+    def columns_in(sweep, j):
+        for k in range(len(peers)):
+            send_y(sweep, j, k).wait_recv()
+        size = padded if sweep == 0 else strip
+        for source in range(rows_count):
+            high, low = split(s.yr[sweep, j, source, 0:size])
+            lanes = slice(source * LANES, (source + 1) * LANES)
+            for n in range(steps):
+                part = slice(n * LANES, (n + 1) * LANES)
+                s.lh[n * size : (n + 1) * size, lanes] = high[:, part]
+                s.ll[n * size : (n + 1) * size, lanes] = low[:, part]
+
+        def tile(i, _):
+            columns = rows_at(i * big, big)
+
+            def right(table):
+                starts = [q * narrow + j * LANES for q in range(rows_count)]
+                return jnp.concatenate([table[a : a + LANES, columns] for a in starts], 0)
+
+            rows = slice(0, steps * size)
+            out = dot3(s.lh[rows], s.ll[rows], right(s.ch), right(s.cl))
+            if sweep == 0:
+                if j > 0:
+                    out = out + s.u1p[:, columns]
+                s.u1p[:, columns] = out
+            else:
+                for n in range(steps):
+                    value = out[n * size : (n + 1) * size]
+                    if j == 0:
+                        value = value + s.w0p[EDGE : EDGE + strip, columns]
+                        value = value + s.u1p[n * padded + EDGE : n * padded + EDGE + strip, columns]
+                    else:
+                        value = value + s.out[n, :, columns]
+                    s.out[n, :, columns] = value
+            return 0
+
+        lax.fori_loop(0, length // big, tile, 0)
+
+    def send_x(j, k):
+        n = j * len(peers) + k
+        target = to(*peers[k])
+        return remote(
+            s.fx.at[j, target],
+            s.xr.at[j, rows_at(r * strip, strip)],
+            s.xs.at[n],
+            s.xrs.at[n],
+            (t, target),
+        )
+
+    def columns_out(j):
+        for dy in list(range(1, ys_count)) + [0]:
+            chip = lax.rem(y + dy, ys_count) * 2
+
+            def right(table):
+                starts = [rows_at((chip + q) * narrow + j * LANES, LANES) for q in range(2)]
+                return jnp.concatenate([table[:, a] for a in starts], 1)
+
+            rows = slice(0, steps * strip)
+            out = dot3(s.ph[rows], s.pl[rows], right(s.cth), right(s.ctl))
+            for q in range(2):
+                for n in range(steps):
+                    s.fx[j, chip + q, :, n * LANES : (n + 1) * LANES] = out[
+                        n * strip : (n + 1) * strip, q * LANES : (q + 1) * LANES
+                    ]
+            for k, peer in enumerate(peers):
+                if peer[0] == dy:
+                    send_x(j, k).start()
+        s.xr[j, rows_at(r * strip, strip)] = s.fx[j, r]
+
+    def gather_x(j):
+        for k in range(len(peers)):
+            send_x(j, k).wait_recv()
+
+        def body(i, _):
+            rows = rows_at(i * LANES, LANES)
+            s.xh[j, rows], s.xl[j, rows] = split(s.xr[j, rows])
+            return 0
+
+        lax.fori_loop(0, length // LANES, body, 0)
+
+    def steady_modes():
+        for k in range(len(peers)):
+            send_d(k).wait_recv()
+
+        def spread(i, _):
+            rows = rows_at(i * LANES, LANES)
+            s.xh[0, rows], s.xl[0, rows] = split(s.xd[rows])
+            return 0
+
+        lax.fori_loop(0, length // LANES, spread, 0)
+
+        def block(i, _):
+            rows = rows_at(i * big, big)
+            out = dot3(s.ch[rows], s.cl[rows], s.xh[0], s.xl[0])
+            for j in range(chunks):
+                s.sd[j, rows] = out[:, j * LANES : (j + 1) * LANES] * s.gw[j, rows]
+            return 0
+
+        lax.fori_loop(0, length // big, block, 0)
+
+    for j in range(chunks):
+        rows_out(0, j)
+    carries(0, 0)
+    steady_modes()
+    for j in range(chunks):
+        if j > 0:
+            carries(0, j)
+        rows_in(0, j)
+    for j in range(chunks):
+        columns_in(0, j)
+    for n in range(steps):
+        offset = n * padded
+
+        @pl.when(r == 0)
+        def _():
+            edge = s.u1p[offset + EDGE : offset + EDGE + 1]
+            s.u1p[offset : offset + EDGE] = jnp.broadcast_to(edge, (EDGE, length))
+
+        @pl.when(r == rows_count - 1)
+        def _():
+            last = offset + EDGE + strip
+            edge = s.u1p[last - 1 : last]
+            s.u1p[last : last + EDGE] = jnp.broadcast_to(edge, (EDGE, length))
+
+        kappa(offset)
+        forcing(offset, n * strip)
+    for j in range(chunks):
+        columns_out(j)
+    gather_x(0)
+    rows_out(1, 0)
+    for j in range(chunks):
+        carries(1, j)
+        if j + 1 < chunks:
+            gather_x(j + 1)
+            rows_out(1, j + 1)
+        rows_in(1, j)
+    for j in range(chunks):
+        columns_in(1, j)
+
+    @pl.when(r < rows_count - 1)
+    def _():
+        halo_down(r + 1).wait_send()
+
+    @pl.when(r > 0)
+    def _():
+        halo_up(r - 1).wait_send()
+
+    for k in range(len(peers)):
+        send_d(k).wait_send()
+        for j in range(chunks):
+            send_x(j, k).wait_send()
+            for sweep in range(ITERS):
+                send_y(sweep, j, k).wait_send()
+    for sweep in range(ITERS):
+        for j in range(chunks):
+
+            def drain(i, _, sweep=sweep, j=j):
+                send_e(sweep, j, i).wait_send()
+                send_c(sweep, j, i).wait_send()
+
+                @pl.when(z < zs - 1)
+                def _():
+                    send_f(sweep, j, i, (t + 2, r)).wait_send()
+
+                @pl.when(z > 0)
+                def _():
+                    send_s(sweep, j, i, (t - 2, r)).wait_send()
+
+                return 0
+
+            lax.fori_loop(0, units, drain, 0)
+
+
+def fused(
+    initial_warmth,
+    pattern_choice,
+    dissipation_tables,
+    material_label,
+    intercept_kappa,
+    sensitivity_coef,
+):
+    steps = pattern_choice.shape[0]
+    strip, length = initial_warmth.shape
+    tm_count, rows_count = lax.axis_size("tm"), lax.axis_size("rows")
+    chunks = length // rows_count // LANES
+    column_cos = cosine_table(length)
+    forward, inverse = two_parts(column_cos.T), two_parts(column_cos)
+    mu = 2.0 - 2.0 * np.cos(np.arange(length) * (math.pi / length))
+    mup = np.broadcast_to(mu[:, None], (length, LANES)).astype(np.float32)
+    muq = np.broadcast_to(mu.reshape(rows_count * chunks, 1, LANES), (rows_count * chunks, 8, LANES))
+    scratch = scratch_of(steps, strip, length, tm_count, rows_count)
+    names = INPUTS + ["out"] + list(scratch)
+    smem, vmem, hbm = (
+        pl.BlockSpec(memory_space=space) for space in (pltpu.SMEM, pltpu.VMEM, pl.ANY)
+    )
+    return pl.pallas_call(
+        lambda *refs: fused_kernel(steps, strip, length, tm_count, rows_count, names, *refs),
+        out_shape=jax.ShapeDtypeStruct((steps, strip, length), F32),
+        in_specs=[vmem, smem, vmem, smem, smem, smem, vmem, vmem] + [hbm] * 4,
+        out_specs=vmem,
+        scratch_shapes=list(scratch.values()),
+        compiler_params=pltpu.CompilerParams(
+            collective_id=0, has_side_effects=True, vmem_limit_bytes=67043328
+        ),
+    )(
+        initial_warmth,
+        pattern_choice,
+        dissipation_tables,
+        material_label,
+        intercept_kappa,
+        sensitivity_coef,
+        jnp.asarray(mup),
+        jnp.asarray(muq.astype(np.float32)),
+        *inverse,
+        *forward,
+    )
+
+
+def pick(initial_warmth, pattern_choice, *rest):
+    strip, width = initial_warmth.shape
+    tm_count, rows_count = lax.axis_size("tm"), lax.axis_size("rows")
+    aligned = (
+        pattern_choice.shape[0] == 2
+        and strip * rows_count == width
+        and strip % TILE == 0
+        and width == rows_count * 2 * LANES
+        and width % (4 * LANES) == 0
+        and tm_count % 2 == 0
+        and rows_count % 2 == 0
+    )
+    return (fused if aligned else shards)(initial_warmth, pattern_choice, *rest)
+
+
 def solution(mesh):
     in_specs = (P("rows", None), P("tm", None, None), P(), P(), P(), P())
     out_specs = P("tm", "rows", None)
-    return jax.shard_map(shards, mesh=mesh, in_specs=in_specs, out_specs=out_specs, check_vma=False)
+    return jax.shard_map(pick, mesh=mesh, in_specs=in_specs, out_specs=out_specs, check_vma=False)

time: 394 us -> 154 us (0.39)
  blocking collectives: 115 us -> 0 us
  waiting for transfers between devices: 95.2 us -> 0 us
  Pallas kernels: 62.7 us -> 150 us
  local copies, waits for them, and re-layouts: 46.5 us -> 3.16 us
  other arithmetic: 39.4 us -> 0 us
  starting transfers between devices: 31 us -> 0 us
    all_to_all x4 -> x0, blocking collectives: 115 us -> none  [the longest x2 58.4 us: shards(): lax.all_to_all(field, 'rows', split_axis=1, concat_axis=2, tiled=True)]
    all_to_all x4 -> x0, waiting for transfers between devices: 95.1 us -> none  [the longest x2 45.9 us: shards(): lax.all_to_all(modes.reshape(steps, strip, width), 'rows', split_axis=2,...]
    pallas_call x9 -> x1, Pallas kernels: 62.7 us -> 150 us  [fused(): pl.pallas_call(lambda *refs: fused_kernel(steps, strip, length, tm_count,...]
    all_to_all x4 -> x0, starting transfers between devices: 18.9 us -> none  [the longest x2 7.33 us: shards(): lax.all_to_all(modes.reshape(steps, strip, width), 'rows', split_axis=2,...]
    add x9 -> x0, other arithmetic: 14.5 us -> none  [the longest x2 5.52 us: shards(): warmth = warmth + update.reshape(steps, strip, width)]
    ppermute x4 -> x0, starting transfers between devices: 12.1 us -> none  [the longest x2 7.14 us: extended(): lax.ppermute(lax.slice_in_dim(block, block.shape[dim] - 1, None, axis=dim...]
    all_to_all x6 -> x0, local copies, waits for them, and re-layouts: 11.5 us -> none  [the longest x4 8.78 us: shards(): lax.all_to_all(modes.reshape(steps, strip, width), 'rows', split_axis=2,...]
    reshape x3 -> x0, local copies, waits for them, and re-layouts: 8.88 us -> none  [the longest x2 8.22 us: shards(): modes.reshape(steps, strip, width)]
  transfers between devices with their start and end apart: 8 -> 0, of which waited for: 5 -> 0; matrix products, arithmetic and copies ran while one was open for 4% -> 0% of each run, Pallas kernels for 1% -> 0%
where the time goes in v1:
time: 154 us; the launch traced here: 153 us
  Pallas kernels  150 us (97%)
  local copies, waits for them, and re-layouts  3.16 us (2%)
    pallas_call x1, Pallas kernels, fused(): pl.pallas_call(lambda *refs: fused_kernel(steps, strip, length, tm_count,...  150 us
    unnamed x1, local copies, waits for them, and re-layouts  3.16 us

profile of v1, /device:TPU:1, one launch (start us, length us, event | category | flops | bytes accessed | tf_op | source)
XLA Modules:
  0.0 153.5 jit_solution(3242260139636305156)
XLA Ops:
  0.0 150.3 %shard_map.118 = f32[2,256,1024]{2,1,0:T(8,128)} custom-call(f32[256,1024]{1,0:T(8,128)} %refs_0_.1, s32[2,8,8]{2,1,0:T(8,128)} %refs_1_.1, f32[8,128,128]{2,1,0:T(8,128)} %refs_2_.1, s32[8,8]{1,0:T(8,128)} %refs_3_.1, f32[4]{0:T(128)} %refs_4_.1, f32[4]{0:T(128)} %refs_5_.1, f32[1024,128]{1,0:T(8,128)} %constant.16.clone.refs_6_, ...), custom_call_target="tpu_custom_call" | custom-call | tf_op jit(solution)/shard_map/pallas_call | solution.py:1063
  150.3 3.2 %copy.14 = f32[2,256,1024]{2,1,0:T(8,128)} copy(f32[2,256,1024]{2,1,0:T(8,128)} %shard_map.118) | data formatting | bytes 4194304

commit v2 on v1

--- a/solution.py
+++ b/solution.py
@@ -272,6 +272,7 @@
 LANES = 128
 EDGE = 8
 ROWS = 32
+UNIT = 64
 MESH = pl.DeviceIdType.MESH
 
 
@@ -294,10 +295,9 @@
     narrow = length // rows_count
     chunks = narrow // LANES
     half = length // 2
-    units = half // LANES
+    units = half // UNIT
     wide = steps * LANES
     padded = strip + 2 * EDGE
-    peers = rows_count - 1
 
     def f32(*shape):
         return pltpu.VMEM(shape, F32)
@@ -321,7 +321,9 @@
         kp=f32(padded, length),
         div0=f32(strip, length),
         halo=f32(2, EDGE, length),
-        dst=f32(peers, strip, narrow),
+        dst=f32(rows_count, strip, narrow),
+        oh=b16(length, narrow),
+        ol=b16(length, narrow),
         xd=f32(length, narrow),
         xh=b16(chunks, length, wide),
         xl=b16(chunks, length, wide),
@@ -335,7 +337,7 @@
         fout=f32(ITERS, chunks, half, LANES),
         sout=f32(ITERS, chunks, half, LANES),
         cs=f32(ITERS, chunks, half, LANES),
-        zz=f32(half, LANES),
+        zz=f32(chunks, half, LANES),
         carry=f32(ITERS, chunks, length, LANES),
         ctot=f32(chunks, length, LANES),
         gw=f32(chunks, length, LANES),
@@ -354,15 +356,17 @@
         lh=b16(steps * padded, rows_count * LANES),
         ll=b16(steps * padded, rows_count * LANES),
         u1p=f32(steps * padded, length),
+        outv=f32(steps, strip, length),
+        osem=dma((length // (2 * LANES),)),
         tsem=dma((4,)),
         hs=dma((2,)),
         hr=dma((2,)),
-        ds=dma((peers,)),
-        dr=dma((peers,)),
-        xs=dma((chunks * peers,)),
-        xrs=dma((chunks * peers,)),
-        ys=dma((ITERS * chunks * peers,)),
-        yrs=dma((ITERS * chunks * peers,)),
+        ds=dma((rows_count,)),
+        dr=dma((rows_count,)),
+        xs=dma((chunks * rows_count,)),
+        xrs=dma((chunks * rows_count,)),
+        ys=dma((ITERS * chunks * rows_count,)),
+        yrs=dma((ITERS * chunks * rows_count,)),
         es=dma((ITERS * chunks * units,)),
         ers=dma((ITERS * chunks * units,)),
         fs=dma((ITERS * chunks * units,)),
@@ -395,7 +399,7 @@
     narrow = length // rows_count
     chunks = narrow // LANES
     half = length // 2
-    units = half // LANES
+    units = half // UNIT
     padded = strip + 2 * EDGE
     blocks = strip // TILE
     tiles = length // TILE
@@ -439,9 +443,6 @@
     def _():
         pl.semaphore_signal(barrier, inc=1, device_id=(t + 2, r), device_id_type=MESH)
 
-    beside = lax.min(z, 1) + lax.min(zs - 1 - z, 1)
-    pl.semaphore_wait(barrier, len(peers) + 1 + beside)
-
     def halo_down(to_row):
         return remote(
             s.w0.at[pl.ds(strip - EDGE, EDGE)], s.halo.at[0], s.hs.at[0], s.hr.at[0], (t, to_row)
@@ -449,14 +450,6 @@
 
     def halo_up(to_row):
         return remote(s.w0.at[pl.ds(0, EDGE)], s.halo.at[1], s.hs.at[1], s.hr.at[1], (t, to_row))
-
-    @pl.when(r < rows_count - 1)
-    def _():
-        halo_down(r + 1).start()
-
-    @pl.when(r > 0)
-    def _():
-        halo_up(r - 1).start()
 
     count = s.icpt.shape[0]
     total = s.icpt[0]
@@ -474,11 +467,11 @@
 
         def factors(i, _, j=j):
             rows = rows_at(i * LANES, LANES)
-            rate = conduct * (s.mup[rows] + CROSS_WEIGHT * s.muq[r * chunks + j, 0:1, :])
+            rate = conduct * (s.mup[rows] + CROSS_WEIGHT * s.muq[j * rows_count + r, 0:1, :])
             gain = 1.0 / (1.0 / TIMESTEP_SIZE + rate)
             keep = gain * (1.0 / TIMESTEP_SIZE)
             p = i * LANES + lax.broadcasted_iota(jnp.int32, (LANES, LANES), 0)
-            q = r * narrow + j * LANES + lax.broadcasted_iota(jnp.int32, (LANES, LANES), 1)
+            q = (j * rows_count + r) * LANES + lax.broadcasted_iota(jnp.int32, (LANES, LANES), 1)
             weight = (jnp.where(p == 0, 1.0, 2.0) / length) * (jnp.where(q == 0, 1.0, 2.0) / length)
             s.gw[j, rows] = gain * weight
             s.keep[j, rows] = keep
@@ -495,8 +488,8 @@
         lax.fori_loop(0, length // LANES, factors, 0)
 
         def chain(i, _, j=j):
-            rows = rows_at(i * LANES, LANES)
-            keep = s.keep[j, rows_at(x * half + i * LANES, LANES)]
+            rows = rows_at(i * UNIT, UNIT)
+            keep = s.keep[j, rows_at(x * half + i * UNIT, UNIT)]
             k = keep * keep
             k2 = k * k
             ones = jnp.ones_like(k)
@@ -529,32 +522,12 @@
     for k in range(s.tables.shape[0]):
         s.th[k], s.tl[k] = split(s.tables[k])
 
-    s.w0p[EDGE : EDGE + strip] = s.w0[...]
-
-    @pl.when(r > 0)
-    def _():
-        halo_down(r).wait_recv()
-        s.w0p[0:EDGE] = s.halo[0]
-
-    @pl.when(r == 0)
-    def _():
-        s.w0p[0:EDGE] = jnp.broadcast_to(s.w0[0:1], (EDGE, length))
-
-    @pl.when(r < rows_count - 1)
-    def _():
-        halo_up(r).wait_recv()
-        s.w0p[EDGE + strip :] = s.halo[1]
-
-    @pl.when(r == rows_count - 1)
-    def _():
-        s.w0p[EDGE + strip :] = jnp.broadcast_to(s.w0[strip - 1 :], (EDGE, length))
-
     def kappa(offset):
         def part(start, size, i):
             rows = pl.ds(start, size)
             warmth = s.w0p[rows]
             if offset is not None:
-                warmth = warmth + s.u1p[pl.ds(offset + start, size)]
+                warmth = warmth + s.u1p[pl.ds(pl.multiple_of(offset + start, EDGE), size)]
             bent = s.slope[i : i + 1] * jnp.tanh(warmth)
             s.kp[rows] = s.base[i : i + 1] * (1.0 + bent)
 
@@ -608,34 +581,32 @@
 
         lax.fori_loop(0, strip // ROWS, inner, 0)
 
-    kappa(None)
-    forcing(None, 0)
+    def send_d(dy, dc):
+        n, target = dy * 2 + dc, to(dy, dc)
+        rows = rows_at(r * strip, strip)
+        return remote(s.dst.at[target], s.xd.at[rows], s.ds.at[n], s.dr.at[n], (t, target))
+
+    beside = lax.min(z, 1) + lax.min(zs - 1 - z, 1)
+    pl.semaphore_wait(barrier, len(peers) + 1 + beside)
+
+    @pl.when(r < rows_count - 1)
+    def _():
+        halo_down(r + 1).start()
+
+    @pl.when(r > 0)
+    def _():
+        halo_up(r - 1).start()
 
     tables_in[0].wait()
     tables_in[1].wait()
 
-    def send_d(k):
-        return remote(
-            s.dst.at[k],
-            s.xd.at[rows_at(r * strip, strip)],
-            s.ds.at[k],
-            s.dr.at[k],
-            (t, to(*peers[k])),
-        )
-
-    for k, peer in enumerate(peers + [(0, 0)]):
-        columns = rows_at(to(*peer) * narrow, narrow)
-        out = dot3(s.ph[0:strip], s.pl[0:strip], s.cth[:, columns], s.ctl[:, columns])
-        if k < len(peers):
-            s.dst[k] = out
-            send_d(k).start()
-        else:
-            s.xd[rows_at(r * strip, strip)] = out
-
-    own = rows_at(r * narrow, narrow)
-    for n in range(steps):
-
-        def place(ty, _, n=n):
+    for j in range(chunks):
+        columns = rows_at((j * rows_count + r) * LANES, LANES)
+        s.oh[:, j * LANES : (j + 1) * LANES] = s.cth[:, columns]
+        s.ol[:, j * LANES : (j + 1) * LANES] = s.ctl[:, columns]
+
+    def power(n, _):
+        def place(ty, _):
             rows = rows_at(ty * TILE, TILE)
             for tx in range(tiles):
                 picked = s.choice[n, ty, tx]
@@ -645,16 +616,20 @@
 
         lax.fori_loop(0, tiles, place, 0)
 
-        def across(i, _, n=n):
+        def across(i, _):
             rows = rows_at(i * half, half)
-            out = dot3(s.ph[rows], s.pl[rows], s.cth[:, own], s.ctl[:, own])
+            out = dot3(s.ph[rows], s.pl[rows], s.oh[...], s.ol[...])
             high, low = split(out)
+            lanes = rows_at(n * LANES, LANES)
             for j in range(chunks):
-                s.xh[j, rows, n * LANES : (n + 1) * LANES] = high[:, j * LANES : (j + 1) * LANES]
-                s.xl[j, rows, n * LANES : (n + 1) * LANES] = low[:, j * LANES : (j + 1) * LANES]
+                s.xh[j, rows, lanes] = high[:, j * LANES : (j + 1) * LANES]
+                s.xl[j, rows, lanes] = low[:, j * LANES : (j + 1) * LANES]
             return 0
 
         lax.fori_loop(0, 2, across, 0)
+        return 0
+
+    lax.fori_loop(0, steps, power, 0)
     tables_in[2].wait()
     tables_in[3].wait()
 
@@ -664,8 +639,8 @@
     def send_e(sweep, j, i):
         n = unit(sweep, j, i)
         return remote(
-            s.e.at[sweep, j, rows_at((1 - x) * half + i * LANES, LANES)],
-            s.er.at[sweep, j, rows_at(i * LANES, LANES)],
+            s.e.at[sweep, j, rows_at((1 - x) * half + i * UNIT, UNIT)],
+            s.er.at[sweep, j, rows_at(i * UNIT, UNIT)],
             s.es.at[n],
             s.ers.at[n],
             (pair, r),
@@ -673,14 +648,14 @@
 
     def send_f(sweep, j, i, device):
         n = unit(sweep, j, i)
-        rows = rows_at(i * LANES, LANES)
+        rows = rows_at(i * UNIT, UNIT)
         return remote(
             s.fout.at[sweep, j, rows], s.fin.at[sweep, j, rows], s.fs.at[n], s.frs.at[n], device
         )
 
     def send_s(sweep, j, i, device):
         n = unit(sweep, j, i)
-        rows = rows_at(i * LANES, LANES)
+        rows = rows_at(i * UNIT, UNIT)
         return remote(
             s.sout.at[sweep, j, rows], s.sin.at[sweep, j, rows], s.gs.at[n], s.grs.at[n], device
         )
@@ -688,8 +663,8 @@
     def send_c(sweep, j, i):
         n = unit(sweep, j, i)
         return remote(
-            s.cs.at[sweep, j, rows_at(i * LANES, LANES)],
-            s.carry.at[sweep, j, rows_at(x * half + i * LANES, LANES)],
+            s.cs.at[sweep, j, rows_at(i * UNIT, UNIT)],
+            s.carry.at[sweep, j, rows_at(x * half + i * UNIT, UNIT)],
             s.cts.at[n],
             s.crs.at[n],
             (pair, r),
@@ -697,13 +672,12 @@
 
     is_first = jnp.where(t == 0, 1.0, 0.0)
 
-    def rows_out(sweep, j):
-        per = big // LANES
+    def rows_out(sweep, j, action=None, beside_j=0):
         parts = length // big
-
-        def block(i, _):
-            b = lax.rem(i + (1 - x) * (parts // 2), parts)
-            rows = rows_at(b * big, big)
+        per = big // UNIT
+
+        def part(i, _):
+            rows = rows_at(lax.rem(i + (1 - x) * (parts // 2), parts) * big, big)
             out = dot3(s.ch[rows], s.cl[rows], s.xh[j], s.xl[j])
             gw, keep = s.gw[j, rows], s.keep[j, rows]
             first, second = out[:, :LANES] * gw, out[:, LANES:] * gw
@@ -718,96 +692,107 @@
                 for n in range(per):
                     send_e(sweep, j, i * per + n).start()
 
-            return 0
-
-        lax.fori_loop(0, parts, block, 0)
-
-    def carries(sweep, j):
-        def halves(i):
-            mine = s.e[sweep, j, rows_at(x * half + i * LANES, LANES)]
-            other = s.er[sweep, j, rows_at(i * LANES, LANES)]
-            return jnp.where(x == 0, mine, other), jnp.where(x == 0, other, mine)
-
-        def pairs(i, _):
-            rows = rows_at(i * LANES, LANES)
-            send_e(sweep, j, i).wait_recv()
-            even, odd = halves(i)
-            block = odd + s.k1[j, rows] * even
-            s.zz[rows] = block
-
-            @pl.when(z == 0)
+            share(action, sweep, beside_j, i, parts)
+            return 0
+
+        lax.fori_loop(0, parts, part, 0)
+
+    def halves(sweep, j, i):
+        mine = s.e[sweep, j, rows_at(x * half + i * UNIT, UNIT)]
+        other = s.er[sweep, j, rows_at(i * UNIT, UNIT)]
+        return jnp.where(x == 0, mine, other), jnp.where(x == 0, other, mine)
+
+    def repeat(sweep, j, *actions):
+        def body(i, _):
+            for action in actions:
+                action(sweep, j, i)
+            return 0
+
+        lax.fori_loop(0, units, body, 0)
+
+    def pair_up(sweep, j, i):
+        rows = rows_at(i * UNIT, UNIT)
+        send_e(sweep, j, i).wait_recv()
+        even, odd = halves(sweep, j, i)
+        block = odd + s.k1[j, rows] * even
+        s.zz[j, rows] = block
+
+        @pl.when(z == 0)
+        def _():
+            s.fout[sweep, j, rows] = block
+            send_f(sweep, j, i, (t + 2, r)).start()
+
+        @pl.when(z == zs - 1)
+        def _():
+            s.sout[sweep, j, rows] = block
+            send_s(sweep, j, i, (t - 2, r)).start()
+
+    def relay_f(sweep, j, i):
+        rows = rows_at(i * UNIT, UNIT)
+
+        @pl.when(z > 0)
+        def _():
+            send_f(sweep, j, i, (t, r)).wait_recv()
+
+            @pl.when(z < zs - 1)
             def _():
-                s.fout[sweep, j, rows] = block
+                s.fout[sweep, j, rows] = s.zz[j, rows] + s.k2[j, rows] * s.fin[sweep, j, rows]
                 send_f(sweep, j, i, (t + 2, r)).start()
 
-            @pl.when(z == zs - 1)
-            def _():
-                s.sout[sweep, j, rows] = block
-                send_s(sweep, j, i, (t - 2, r)).start()
-
-            return 0
-
-        lax.fori_loop(0, units, pairs, 0)
-
-        def relay_f(i):
-            rows = rows_at(i * LANES, LANES)
+    def relay_s(sweep, j, i):
+        rows = rows_at(i * UNIT, UNIT)
+
+        @pl.when(z < zs - 1)
+        def _():
+            send_s(sweep, j, i, (t, r)).wait_recv()
+            s.sout[sweep, j, rows] = s.sin[sweep, j, rows] + s.pa[j, rows] * s.zz[j, rows]
 
             @pl.when(z > 0)
             def _():
-                send_f(sweep, j, i, (t, r)).wait_recv()
-
-                @pl.when(z < zs - 1)
-                def _():
-                    s.fout[sweep, j, rows] = s.zz[rows] + s.k2[j, rows] * s.fin[sweep, j, rows]
-                    send_f(sweep, j, i, (t + 2, r)).start()
-
-        def relay_s(i):
-            rows = rows_at(i * LANES, LANES)
-
-            @pl.when(z < zs - 1)
-            def _():
-                send_s(sweep, j, i, (t, r)).wait_recv()
-                s.sout[sweep, j, rows] = s.sin[sweep, j, rows] + s.pa[j, rows] * s.zz[rows]
-
-                @pl.when(z > 0)
-                def _():
-                    send_s(sweep, j, i, (t - 2, r)).start()
-
-        def finish(i):
-            rows = rows_at(i * LANES, LANES)
-            even, _ = halves(i)
-            lower = s.fin[sweep, j, rows] * s.pf[j, rows] + s.pb[j, rows] * s.sout[sweep, j, rows]
-            upper = even + s.k1[j, rows] * lower
-            s.carry[sweep, j, rows_at(x * half + i * LANES, LANES)] = jnp.where(
-                x == 0, lower, upper
-            )
-            s.cs[sweep, j, rows] = jnp.where(x == 0, upper, lower)
-            send_c(sweep, j, i).start()
-
-        def run(first, second):
-            def one(i, _):
-                first(i)
-                return 0
-
-            def two(i, _):
-                second(i)
-                finish(i)
-                return 0
-
-            lax.fori_loop(0, units, one, 0)
-            lax.fori_loop(0, units, two, 0)
-
+                send_s(sweep, j, i, (t - 2, r)).start()
+
+    def finish(sweep, j, i):
+        rows = rows_at(i * UNIT, UNIT)
+        even, _ = halves(sweep, j, i)
+        lower = s.fin[sweep, j, rows] * s.pf[j, rows] + s.pb[j, rows] * s.sout[sweep, j, rows]
+        upper = even + s.k1[j, rows] * lower
+        s.carry[sweep, j, rows_at(x * half + i * UNIT, UNIT)] = jnp.where(x == 0, lower, upper)
+        s.cs[sweep, j, rows] = jnp.where(x == 0, upper, lower)
+        send_c(sweep, j, i).start()
+
+    def relay_near(sweep, j, i):
         @pl.when(z < zs // 2)
         def _():
-            run(relay_f, relay_s)
+            relay_f(sweep, j, i)
 
         @pl.when(z >= zs // 2)
         def _():
-            run(relay_s, relay_f)
-
-    def send_y(sweep, j, k):
-        n = (sweep * chunks + j) * len(peers) + k
-        target = to(*peers[k])
+            relay_s(sweep, j, i)
+
+    def relay_away(sweep, j, i):
+        @pl.when(z < zs // 2)
+        def _():
+            relay_s(sweep, j, i)
+
+        @pl.when(z >= zs // 2)
+        def _():
+            relay_f(sweep, j, i)
+
+        finish(sweep, j, i)
+
+    def some(action, sweep, j, first, last):
+        def body(i, _):
+            action(sweep, j, i)
+            return 0
+
+        lax.fori_loop(first, last, body, 0)
+
+    def share(action, sweep, j, i, parts):
+        if action is not None:
+            some(action, sweep, j, i * (units // parts), (i + 1) * (units // parts))
+
+    def send_y(sweep, j, dy, dc):
+        n, target = (sweep * chunks + j) * rows_count + dy * 2 + dc, to(dy, dc)
         size = padded if sweep == 0 else strip
         start = target * strip if sweep == 0 else target * strip + EDGE
         return remote(
@@ -818,12 +803,8 @@
             (t, target),
         )
 
-    def rows_in(sweep, j):
-        def wait(i, _):
-            send_c(sweep, j, i).wait_recv()
-            return 0
-
-        lax.fori_loop(0, units, wait, 0)
+    def rows_in(sweep, j, action=None):
+        some(lambda *which: send_c(*which).wait_recv(), sweep, j, 0, units)
 
         def solve(i, _):
             rows = rows_at(i * LANES, LANES)
@@ -842,101 +823,114 @@
 
         lax.fori_loop(0, length // LANES, solve, 0)
 
-        def block(target):
+        def part(i, _):
+            dy, q = lax.rem(lax.div(i, 2) + 1, ys_count), lax.rem(i, 2)
+            target = lax.rem(y + dy, ys_count) * 2 + q
             rows = rows_at(target * strip, strip)
             out = dot3(s.cth[rows], s.ctl[rows], s.uh[...], s.ul[...])
             s.iy[sweep, j, pl.ds(pl.multiple_of(target * strip + EDGE, EDGE), strip)] = out
-
+            if sweep > 0:
+
+                @pl.when(target != r)
+                def _():
+                    send_y(sweep, j, dy, lax.rem(q + c, 2)).start()
+
+            share(action, sweep, j + 1, i, rows_count)
+            return 0
+
+        lax.fori_loop(0, rows_count, part, 0)
         if sweep == 0:
-
-            def body(i, _):
-                block(i)
-                return 0
-
-            lax.fori_loop(0, rows_count, body, 0)
-            for k in range(len(peers)):
-                send_y(sweep, j, k).start()
+            for dy, dc in peers:
+                send_y(sweep, j, dy, dc).start()
             s.yr[sweep, j, r] = s.iy[sweep, j, pl.ds(pl.multiple_of(r * strip, EDGE), padded)]
         else:
-            for k, peer in enumerate(peers):
-                block(to(*peer))
-                send_y(sweep, j, k).start()
-            block(r)
             mid = pl.ds(pl.multiple_of(r * strip + EDGE, EDGE), strip)
             s.yr[sweep, j, r, 0:strip] = s.iy[sweep, j, mid]
 
-    def columns_in(sweep, j):
-        for k in range(len(peers)):
-            send_y(sweep, j, k).wait_recv()
+    def store(i):
+        columns = rows_at(i * big, big)
+        return pltpu.make_async_copy(
+            s.outv.at[:, :, columns], s.out.at[:, :, columns], s.osem.at[i]
+        )
+
+    def columns_in(sweep):
         size = padded if sweep == 0 else strip
-        for source in range(rows_count):
-            high, low = split(s.yr[sweep, j, source, 0:size])
-            lanes = slice(source * LANES, (source + 1) * LANES)
-            for n in range(steps):
-                part = slice(n * LANES, (n + 1) * LANES)
-                s.lh[n * size : (n + 1) * size, lanes] = high[:, part]
-                s.ll[n * size : (n + 1) * size, lanes] = low[:, part]
-
-        def tile(i, _):
-            columns = rows_at(i * big, big)
-
-            def right(table):
-                starts = [q * narrow + j * LANES for q in range(rows_count)]
-                return jnp.concatenate([table[a : a + LANES, columns] for a in starts], 0)
-
-            rows = slice(0, steps * size)
-            out = dot3(s.lh[rows], s.ll[rows], right(s.ch), right(s.cl))
-            if sweep == 0:
-                if j > 0:
-                    out = out + s.u1p[:, columns]
-                s.u1p[:, columns] = out
-            else:
+
+        def chunk(j, _):
+            for dy, dc in peers:
+                send_y(sweep, j, dy, dc).wait_recv()
+            for source in range(rows_count):
+                high, low = split(s.yr[sweep, j, source, 0:size])
+                lanes = slice(source * LANES, (source + 1) * LANES)
                 for n in range(steps):
-                    value = out[n * size : (n + 1) * size]
-                    if j == 0:
-                        value = value + s.w0p[EDGE : EDGE + strip, columns]
-                        value = value + s.u1p[n * padded + EDGE : n * padded + EDGE + strip, columns]
-                    else:
-                        value = value + s.out[n, :, columns]
-                    s.out[n, :, columns] = value
-            return 0
-
-        lax.fori_loop(0, length // big, tile, 0)
-
-    def send_x(j, k):
-        n = j * len(peers) + k
-        target = to(*peers[k])
+                    part = slice(n * LANES, (n + 1) * LANES)
+                    s.lh[n * size : (n + 1) * size, lanes] = high[:, part]
+                    s.ll[n * size : (n + 1) * size, lanes] = low[:, part]
+
+            def tile(i, _):
+                columns = rows_at(i * big, big)
+                depth = rows_at(j * rows_count * LANES, rows_count * LANES)
+                rows = slice(0, steps * size)
+                out = dot3(s.lh[rows], s.ll[rows], s.ch[depth, columns], s.cl[depth, columns])
+                if sweep == 0:
+                    s.u1p[:, columns] = s.u1p[:, columns] + out
+                else:
+                    for n in range(steps):
+                        value = s.outv[n, :, columns] + out[n * size : (n + 1) * size]
+                        s.outv[n, :, columns] = value
+
+                    @pl.when(j == chunks - 1)
+                    def _():
+                        store(i).start()
+
+                return 0
+
+            lax.fori_loop(0, length // big, tile, 0)
+            return 0
+
+        lax.fori_loop(0, chunks, chunk, 0)
+
+    def send_x(j, dy, dc):
+        n, target = j * rows_count + dy * 2 + dc, to(dy, dc)
+        rows = rows_at(r * strip, strip)
         return remote(
-            s.fx.at[j, target],
-            s.xr.at[j, rows_at(r * strip, strip)],
-            s.xs.at[n],
-            s.xrs.at[n],
-            (t, target),
+            s.fx.at[j, target], s.xr.at[j, rows], s.xs.at[n], s.xrs.at[n], (t, target)
         )
 
-    def columns_out(j):
-        for dy in list(range(1, ys_count)) + [0]:
+    def send_chip(send, dy):
+        for q in range(2):
+            dc = lax.rem(q + c, 2)
+
+            @pl.when(dy * 2 + dc > 0)
+            def _():
+                send(dy, dc).start()
+
+    def columns_out():
+        def part(i, _):
+            n, g = lax.rem(i, steps), lax.div(i, steps)
+            dy, j = lax.rem(g + 1, ys_count), lax.div(g, ys_count)
             chip = lax.rem(y + dy, ys_count) * 2
-
-            def right(table):
-                starts = [rows_at((chip + q) * narrow + j * LANES, LANES) for q in range(2)]
-                return jnp.concatenate([table[:, a] for a in starts], 1)
-
-            rows = slice(0, steps * strip)
-            out = dot3(s.ph[rows], s.pl[rows], right(s.cth), right(s.ctl))
+            rows = rows_at(n * strip, strip)
+            columns = rows_at((j * rows_count + chip) * LANES, big)
+            out = dot3(s.ph[rows], s.pl[rows], s.cth[:, columns], s.ctl[:, columns])
             for q in range(2):
-                for n in range(steps):
-                    s.fx[j, chip + q, :, n * LANES : (n + 1) * LANES] = out[
-                        n * strip : (n + 1) * strip, q * LANES : (q + 1) * LANES
-                    ]
-            for k, peer in enumerate(peers):
-                if peer[0] == dy:
-                    send_x(j, k).start()
-        s.xr[j, rows_at(r * strip, strip)] = s.fx[j, r]
+                s.fx[j, chip + q, :, rows_at(n * LANES, LANES)] = out[
+                    :, q * LANES : (q + 1) * LANES
+                ]
+
+            @pl.when(n == steps - 1)
+            def _():
+                send_chip(lambda *to_: send_x(j, *to_), dy)
+
+            return 0
+
+        lax.fori_loop(0, chunks * ys_count * steps, part, 0)
 
     def gather_x(j):
-        for k in range(len(peers)):
-            send_x(j, k).wait_recv()
+        own = rows_at(r * strip, strip)
+        s.xr[j, own] = s.fx[j, r]
+        for dy, dc in peers:
+            send_x(j, dy, dc).wait_recv()
 
         def body(i, _):
             rows = rows_at(i * LANES, LANES)
@@ -945,9 +939,51 @@
 
         lax.fori_loop(0, length // LANES, body, 0)
 
-    def steady_modes():
-        for k in range(len(peers)):
-            send_d(k).wait_recv()
+    def steady_out(action, sweep, beside_j):
+        s.w0p[EDGE : EDGE + strip] = s.w0[...]
+
+        @pl.when(r > 0)
+        def _():
+            halo_down(r).wait_recv()
+            s.w0p[0:EDGE] = s.halo[0]
+
+        @pl.when(r == 0)
+        def _():
+            s.w0p[0:EDGE] = jnp.broadcast_to(s.w0[0:1], (EDGE, length))
+
+        @pl.when(r < rows_count - 1)
+        def _():
+            halo_up(r).wait_recv()
+            s.w0p[EDGE + strip :] = s.halo[1]
+
+        @pl.when(r == rows_count - 1)
+        def _():
+            s.w0p[EDGE + strip :] = jnp.broadcast_to(s.w0[strip - 1 :], (EDGE, length))
+
+        kappa(None)
+        forcing(None, 0)
+
+        def part(i, _):
+            j, dy = lax.rem(i, chunks), lax.rem(lax.div(i, chunks) + 1, ys_count)
+            chip = lax.rem(y + dy, ys_count) * 2
+            columns = rows_at((j * rows_count + chip) * LANES, big)
+            out = dot3(s.ph[0:strip], s.pl[0:strip], s.cth[:, columns], s.ctl[:, columns])
+            for q in range(2):
+                s.dst[chip + q, :, rows_at(j * LANES, LANES)] = out[:, q * LANES : (q + 1) * LANES]
+
+            @pl.when(j == chunks - 1)
+            def _():
+                send_chip(send_d, dy)
+
+            share(action, sweep, beside_j, i, chunks * ys_count)
+            return 0
+
+        lax.fori_loop(0, chunks * ys_count, part, 0)
+        s.xd[rows_at(r * strip, strip)] = s.dst[r]
+
+    def steady_in():
+        for dy, dc in peers:
+            send_d(dy, dc).wait_recv()
 
         def spread(i, _):
             rows = rows_at(i * LANES, LANES)
@@ -965,44 +1001,55 @@
 
         lax.fori_loop(0, length // big, block, 0)
 
-    for j in range(chunks):
-        rows_out(0, j)
-    carries(0, 0)
-    steady_modes()
-    for j in range(chunks):
-        if j > 0:
-            carries(0, j)
-        rows_in(0, j)
-    for j in range(chunks):
-        columns_in(0, j)
-    for n in range(steps):
+    rows_out(0, 0)
+    steady_out(pair_up, 0, 0)
+    rows_out(0, 1, relay_near, 0)
+    some(relay_away, 0, 0, 0, units)
+    some(pair_up, 0, 1, 0, units)
+    steady_in()
+    rows_in(0, 0, relay_near)
+    some(relay_away, 0, 1, 0, units)
+    rows_in(0, 1)
+    s.u1p[...] = jnp.zeros_like(s.u1p)
+    columns_in(0)
+
+    def force(n, _):
         offset = n * padded
 
         @pl.when(r == 0)
         def _():
-            edge = s.u1p[offset + EDGE : offset + EDGE + 1]
-            s.u1p[offset : offset + EDGE] = jnp.broadcast_to(edge, (EDGE, length))
+            edge = s.u1p[pl.ds(pl.multiple_of(offset + EDGE, EDGE), EDGE)][0:1]
+            home = pl.ds(pl.multiple_of(offset, EDGE), EDGE)
+            s.u1p[home] = jnp.broadcast_to(edge, (EDGE, length))
 
         @pl.when(r == rows_count - 1)
         def _():
-            last = offset + EDGE + strip
-            edge = s.u1p[last - 1 : last]
-            s.u1p[last : last + EDGE] = jnp.broadcast_to(edge, (EDGE, length))
+            edge = s.u1p[pl.ds(pl.multiple_of(offset + strip, EDGE), EDGE)][EDGE - 1 :]
+            home = pl.ds(pl.multiple_of(offset + strip + EDGE, EDGE), EDGE)
+            s.u1p[home] = jnp.broadcast_to(edge, (EDGE, length))
 
         kappa(offset)
         forcing(offset, n * strip)
-    for j in range(chunks):
-        columns_out(j)
+        return 0
+
+    lax.fori_loop(0, steps, force, 0)
+    columns_out()
+    for n in range(steps):
+        first = n * padded + EDGE
+        s.outv[n] = s.w0[...] + s.u1p[first : first + strip]
     gather_x(0)
     rows_out(1, 0)
-    for j in range(chunks):
-        carries(1, j)
-        if j + 1 < chunks:
-            gather_x(j + 1)
-            rows_out(1, j + 1)
-        rows_in(1, j)
-    for j in range(chunks):
-        columns_in(1, j)
+    some(pair_up, 1, 0, 0, units)
+    some(relay_near, 1, 0, 0, units)
+    gather_x(1)
+    rows_out(1, 1, relay_away, 0)
+    some(pair_up, 1, 1, 0, units)
+    rows_in(1, 0, relay_near)
+    some(relay_away, 1, 1, 0, units)
+    rows_in(1, 1)
+    columns_in(1)
+    for i in range(length // big):
+        store(i).wait()
 
     @pl.when(r < rows_count - 1)
     def _():
@@ -1012,12 +1059,12 @@
     def _():
         halo_up(r - 1).wait_send()
 
-    for k in range(len(peers)):
-        send_d(k).wait_send()
+    for dy, dc in peers:
+        send_d(dy, dc).wait_send()
         for j in range(chunks):
-            send_x(j, k).wait_send()
+            send_x(j, dy, dc).wait_send()
             for sweep in range(ITERS):
-                send_y(sweep, j, k).wait_send()
+                send_y(sweep, j, dy, dc).wait_send()
     for sweep in range(ITERS):
         for j in range(chunks):
 
@@ -1064,7 +1111,7 @@
         lambda *refs: fused_kernel(steps, strip, length, tm_count, rows_count, names, *refs),
         out_shape=jax.ShapeDtypeStruct((steps, strip, length), F32),
         in_specs=[vmem, smem, vmem, smem, smem, smem, vmem, vmem] + [hbm] * 4,
-        out_specs=vmem,
+        out_specs=hbm,
         scratch_shapes=list(scratch.values()),
         compiler_params=pltpu.CompilerParams(
             collective_id=0, has_side_effects=True, vmem_limit_bytes=67043328

time: 154 us -> 140 us (0.909)
  Pallas kernels: 150 us -> 137 us
    pallas_call x1, Pallas kernels: 150 us -> 137 us  [fused(): pl.pallas_call(lambda *refs: fused_kernel(steps, strip, length, tm_count,...]
where the time goes in v2:
time: 140 us
  Pallas kernels  137 us (98%)
  local copies, waits for them, and re-layouts  3.16 us (2%)
    pallas_call x1, Pallas kernels, fused(): pl.pallas_call(lambda *refs: fused_kernel(steps, strip, length, tm_count,...  137 us
    unnamed x1, local copies, waits for them, and re-layouts  3.16 us

profile of v2, /device:TPU:1, one launch (start us, length us, event | category | flops | bytes accessed | tf_op | source)
XLA Modules:
  0.0 140.3 jit_solution(15862406469501081986)
XLA Ops:
  0.0 137.2 %shard_map.118 = f32[2,256,1024]{2,1,0:T(8,128)} custom-call(f32[256,1024]{1,0:T(8,128)} %refs_0_.1, s32[2,8,8]{2,1,0:T(8,128)} %refs_1_.1, f32[8,128,128]{2,1,0:T(8,128)} %refs_2_.1, s32[8,8]{1,0:T(8,128)} %refs_3_.1, f32[4]{0:T(128)} %refs_4_.1, f32[4]{0:T(128)} %refs_5_.1, f32[1024,128]{1,0:T(8,128)} %constant.16.clone.refs_6_, ...), custom_call_target="tpu_custom_call" | custom-call | tf_op jit(solution)/shard_map/pallas_call | solution.py:1110
  137.2 3.2 %copy.14 = f32[2,256,1024]{2,1,0:T(8,128)} copy(f32[2,256,1024]{2,1,0:T(8,128)} %shard_map.118) | data formatting | bytes 4194304

commit v3 on v2

--- a/solution.py
+++ b/solution.py
@@ -319,7 +319,6 @@
         slope=f32(8, length),
         w0p=f32(padded, length),
         kp=f32(padded, length),
-        div0=f32(strip, length),
         halo=f32(2, EDGE, length),
         dst=f32(rows_count, strip, narrow),
         oh=b16(length, narrow),
@@ -339,7 +338,6 @@
         cs=f32(ITERS, chunks, half, LANES),
         zz=f32(chunks, half, LANES),
         carry=f32(ITERS, chunks, length, LANES),
-        ctot=f32(chunks, length, LANES),
         gw=f32(chunks, length, LANES),
         keep=f32(chunks, length, LANES),
         rho=f32(chunks, length, LANES),
@@ -367,14 +365,14 @@
         xrs=dma((chunks * rows_count,)),
         ys=dma((ITERS * chunks * rows_count,)),
         yrs=dma((ITERS * chunks * rows_count,)),
-        es=dma((ITERS * chunks * units,)),
-        ers=dma((ITERS * chunks * units,)),
-        fs=dma((ITERS * chunks * units,)),
-        frs=dma((ITERS * chunks * units,)),
-        gs=dma((ITERS * chunks * units,)),
-        grs=dma((ITERS * chunks * units,)),
-        cts=dma((ITERS * chunks * units,)),
-        crs=dma((ITERS * chunks * units,)),
+        es=dma((ITERS * chunks,)),
+        ers=dma((chunks * units,)),
+        fs=dma((ITERS * chunks,)),
+        frs=dma((chunks * units,)),
+        gs=dma((ITERS * chunks,)),
+        grs=dma((chunks * units,)),
+        cts=dma((ITERS * chunks,)),
+        crs=dma((chunks * units,)),
     )
 
 
@@ -463,9 +461,9 @@
             s.base[i : i + 1, tx * TILE : (tx + 1) * TILE] = jnp.full((1, TILE), s.icpt[label], F32)
             s.slope[i : i + 1, tx * TILE : (tx + 1) * TILE] = jnp.full((1, TILE), s.sens[label], F32)
 
-    for j in range(chunks):
-
-        def factors(i, _, j=j):
+    def factors_of(j):
+
+        def factors(i, _):
             rows = rows_at(i * LANES, LANES)
             rate = conduct * (s.mup[rows] + CROSS_WEIGHT * s.muq[j * rows_count + r, 0:1, :])
             gain = 1.0 / (1.0 / TIMESTEP_SIZE + rate)
@@ -487,7 +485,7 @@
 
         lax.fori_loop(0, length // LANES, factors, 0)
 
-        def chain(i, _, j=j):
+        def chain(i, _):
             rows = rows_at(i * UNIT, UNIT)
             keep = s.keep[j, rows_at(x * half + i * UNIT, UNIT)]
             k = keep * keep
@@ -508,6 +506,8 @@
 
         lax.fori_loop(0, units, chain, 0)
 
+    factors_of(0)
+
     @pl.when(z == 0)
     def _():
         s.fin[...] = jnp.zeros_like(s.fin)
@@ -550,31 +550,16 @@
             warmth, k = s.w0p[rows], s.kp[rows]
             mid = slice(EDGE, EDGE + ROWS)
             if offset is not None:
-                u = s.u1p[pl.ds(pl.multiple_of(offset + i * ROWS, EDGE), ext)]
-                warmth = warmth + u
-
-            def flux(shift, w, k, u):
-                value = 0.5 * (k + shift(k)) * (shift(w) - w)
-                if u is not None:
-                    value = value - conduct * (shift(u) - u)
-                return value
-
-            u = u if offset is not None else None
-            down = flux(lambda v: pltpu.roll(v, ext - 1, 0), warmth, k, u)
+                warmth = warmth + s.u1p[pl.ds(pl.multiple_of(offset + i * ROWS, EDGE), ext)]
+
+            def flux(shift, w, k):
+                return 0.5 * (k + shift(k)) * (shift(w) - w)
+
+            down = flux(lambda v: pltpu.roll(v, ext - 1, 0), warmth, k)
             total = (down - pltpu.roll(down, 1, 0))[mid]
-            right = flux(
-                lambda v: pltpu.roll(v, length - 1, 1),
-                warmth[mid],
-                k[mid],
-                None if u is None else u[mid],
-            )
+            right = flux(lambda v: pltpu.roll(v, length - 1, 1), warmth[mid], k[mid])
             right = jnp.where(lane < length - 1, right, 0.0)
             total = total + CROSS_WEIGHT * (right - pltpu.roll(right, 1, 1))
-            home = pl.ds(pl.multiple_of(i * ROWS, ROWS), ROWS)
-            if offset is None:
-                s.div0[home] = total
-            else:
-                total = total - s.div0[home]
             rows = pl.ds(pl.multiple_of(out_row + i * ROWS, ROWS), ROWS)
             s.ph[rows], s.pl[rows] = split(total)
             return 0
@@ -634,45 +619,45 @@
     tables_in[3].wait()
 
     def unit(sweep, j, i):
-        return (sweep * chunks + j) * units + i
-
-    def send_e(sweep, j, i):
+        return j * units + i
+
+    def send_e(sweep, j, i, size=UNIT):
         n = unit(sweep, j, i)
         return remote(
-            s.e.at[sweep, j, rows_at((1 - x) * half + i * UNIT, UNIT)],
-            s.er.at[sweep, j, rows_at(i * UNIT, UNIT)],
-            s.es.at[n],
+            s.e.at[sweep, j, rows_at((1 - x) * half + i * size, size)],
+            s.er.at[sweep, j, rows_at(i * size, size)],
+            s.es.at[sweep * chunks + j],
             s.ers.at[n],
             (pair, r),
         )
 
-    def send_f(sweep, j, i, device):
+    def send_f(sweep, j, i, device, size=UNIT):
         n = unit(sweep, j, i)
-        rows = rows_at(i * UNIT, UNIT)
+        rows = rows_at(i * size, size)
         return remote(
-            s.fout.at[sweep, j, rows], s.fin.at[sweep, j, rows], s.fs.at[n], s.frs.at[n], device
+            s.fout.at[sweep, j, rows], s.fin.at[sweep, j, rows], s.fs.at[sweep * chunks + j], s.frs.at[n], device
         )
 
-    def send_s(sweep, j, i, device):
+    def send_s(sweep, j, i, device, size=UNIT):
         n = unit(sweep, j, i)
-        rows = rows_at(i * UNIT, UNIT)
+        rows = rows_at(i * size, size)
         return remote(
-            s.sout.at[sweep, j, rows], s.sin.at[sweep, j, rows], s.gs.at[n], s.grs.at[n], device
+            s.sout.at[sweep, j, rows], s.sin.at[sweep, j, rows], s.gs.at[sweep * chunks + j], s.grs.at[n], device
         )
 
-    def send_c(sweep, j, i):
+    def send_c(sweep, j, i, size=UNIT):
         n = unit(sweep, j, i)
         return remote(
-            s.cs.at[sweep, j, rows_at(i * UNIT, UNIT)],
-            s.carry.at[sweep, j, rows_at(x * half + i * UNIT, UNIT)],
-            s.cts.at[n],
+            s.cs.at[sweep, j, rows_at(i * size, size)],
+            s.carry.at[sweep, j, rows_at(x * half + i * size, size)],
+            s.cts.at[sweep * chunks + j],
             s.crs.at[n],
             (pair, r),
         )
 
     is_first = jnp.where(t == 0, 1.0, 0.0)
 
-    def rows_out(sweep, j, action=None, beside_j=0):
+    def rows_out(sweep, j, action=None, beside_j=0, at_once=False):
         parts = length // big
         per = big // UNIT
 
@@ -682,7 +667,8 @@
             gw, keep = s.gw[j, rows], s.keep[j, rows]
             first, second = out[:, :LANES] * gw, out[:, LANES:] * gw
             if sweep > 0:
-                first = first - is_first * keep * s.ctot[j, rows]
+                first = first + s.ss[j, rows, :LANES]
+                second = second + s.ss[j, rows, LANES:]
             s.ss[j, rows, :LANES] = first
             s.ss[j, rows, LANES:] = second
             s.e[sweep, j, rows] = second + keep * first
@@ -692,7 +678,13 @@
                 for n in range(per):
                     send_e(sweep, j, i * per + n).start()
 
-            share(action, sweep, beside_j, i, parts)
+            if at_once:
+
+                @pl.when(i == 0)
+                def _():
+                    some(action, sweep, beside_j, 0, units)
+            else:
+                share(action, sweep, beside_j, i, parts)
             return 0
 
         lax.fori_loop(0, parts, part, 0)
@@ -790,6 +782,17 @@
     def share(action, sweep, j, i, parts):
         if action is not None:
             some(action, sweep, j, i * (units // parts), (i + 1) * (units // parts))
+
+    inner = (z > 0) & (z < zs - 1)
+
+    def by_place(relaying, ending):
+        @pl.when(inner)
+        def _():
+            relaying()
+
+        @pl.when(jnp.logical_not(inner))
+        def _():
+            ending()
 
     def send_y(sweep, j, dy, dc):
         n, target = (sweep * chunks + j) * rows_count + dy * 2 + dc, to(dy, dc)
@@ -814,9 +817,12 @@
                 steady = s.sd[j, rows]
                 first, second = first + steady, second + steady
                 carry = carry + s.rho[j, rows] * steady
-                s.ctot[j, rows] = carry
             first = first + keep * carry
             second = second + keep * first
+            if sweep == 0:
+                left = (1.0 - keep) * first - steady
+                s.ss[j, rows, :LANES] = left - is_first * keep * carry
+                s.ss[j, rows, LANES:] = (1.0 - keep) * second - steady
             s.uh[rows, :LANES], s.ul[rows, :LANES] = split(first)
             s.uh[rows, LANES:], s.ul[rows, LANES:] = split(second)
             return 0
@@ -1002,6 +1008,8 @@
         lax.fori_loop(0, length // big, block, 0)
 
     rows_out(0, 0)
+    for j in range(1, chunks):
+        factors_of(j)
     steady_out(pair_up, 0, 0)
     rows_out(0, 1, relay_near, 0)
     some(relay_away, 0, 0, 0, units)
@@ -1041,16 +1049,21 @@
     rows_out(1, 0)
     some(pair_up, 1, 0, 0, units)
     some(relay_near, 1, 0, 0, units)
-    gather_x(1)
-    rows_out(1, 1, relay_away, 0)
+
+    def relay_then_rows():
+        some(relay_away, 1, 0, 0, units)
+        gather_x(1)
+        rows_out(1, 1)
+
+    def rows_then_end():
+        gather_x(1)
+        rows_out(1, 1, relay_away, 0, at_once=True)
+
+    by_place(relay_then_rows, rows_then_end)
     some(pair_up, 1, 1, 0, units)
     rows_in(1, 0, relay_near)
     some(relay_away, 1, 1, 0, units)
     rows_in(1, 1)
-    columns_in(1)
-    for i in range(length // big):
-        store(i).wait()
-
     @pl.when(r < rows_count - 1)
     def _():
         halo_down(r + 1).wait_send()
@@ -1063,26 +1076,62 @@
         send_d(dy, dc).wait_send()
         for j in range(chunks):
             send_x(j, dy, dc).wait_send()
-            for sweep in range(ITERS):
-                send_y(sweep, j, dy, dc).wait_send()
+            send_y(0, j, dy, dc).wait_send()
     for sweep in range(ITERS):
         for j in range(chunks):
-
-            def drain(i, _, sweep=sweep, j=j):
-                send_e(sweep, j, i).wait_send()
-                send_c(sweep, j, i).wait_send()
-
-                @pl.when(z < zs - 1)
-                def _():
-                    send_f(sweep, j, i, (t + 2, r)).wait_send()
-
-                @pl.when(z > 0)
-                def _():
-                    send_s(sweep, j, i, (t - 2, r)).wait_send()
-
-                return 0
-
-            lax.fori_loop(0, units, drain, 0)
+            send_e(sweep, j, 0, half).wait_send()
+            send_c(sweep, j, 0, half).wait_send()
+
+            @pl.when(z < zs - 1)
+            def _():
+                send_f(sweep, j, 0, (t + 2, r), half).wait_send()
+
+            @pl.when(z > 0)
+            def _():
+                send_s(sweep, j, 0, (t - 2, r), half).wait_send()
+    columns_in(1)
+    for i in range(length // big):
+        store(i).wait()
+    for dy, dc in peers:
+        for j in range(chunks):
+            send_y(1, j, dy, dc).wait_send()
+
+
+def pass_on_kernel(in_ref, out_ref, held, in_sem, out_sem):
+    count = in_sem.shape[0]
+    rows = in_ref.shape[0] // count
+
+    def part(i):
+        return pl.ds(i * rows, rows)
+
+    loads = [
+        pltpu.make_async_copy(in_ref.at[part(i)], held.at[part(i)], in_sem.at[i])
+        for i in range(count)
+    ]
+    stores = [
+        pltpu.make_async_copy(held.at[part(i)], out_ref.at[part(i)], out_sem.at[i])
+        for i in range(count)
+    ]
+    for load in loads:
+        load.start()
+    for load, store in zip(loads, stores):
+        load.wait()
+        store.start()
+    for store in stores:
+        store.wait()
+
+
+def pass_on(values, parts=8):
+    flat = values.reshape(-1, values.shape[-1])
+    hbm = pl.BlockSpec(memory_space=pl.ANY)
+    dma = pltpu.SemaphoreType.DMA
+    return pl.pallas_call(
+        pass_on_kernel,
+        out_shape=jax.ShapeDtypeStruct(flat.shape, flat.dtype),
+        in_specs=[hbm],
+        out_specs=hbm,
+        scratch_shapes=[pltpu.VMEM(flat.shape, flat.dtype), dma((parts,)), dma((parts,))],
+    )(flat).reshape(values.shape)
 
 
 def fused(
@@ -1107,7 +1156,7 @@
     smem, vmem, hbm = (
         pl.BlockSpec(memory_space=space) for space in (pltpu.SMEM, pltpu.VMEM, pl.ANY)
     )
-    return pl.pallas_call(
+    result = pl.pallas_call(
         lambda *refs: fused_kernel(steps, strip, length, tm_count, rows_count, names, *refs),
         out_shape=jax.ShapeDtypeStruct((steps, strip, length), F32),
         in_specs=[vmem, smem, vmem, smem, smem, smem, vmem, vmem] + [hbm] * 4,
@@ -1128,6 +1177,7 @@
         *inverse,
         *forward,
     )
+    return pass_on(result)
 
 
 def pick(initial_warmth, pattern_choice, *rest):

time: 140 us -> 137 us (0.979)
  local copies, waits for them, and re-layouts: 3.16 us -> 0 us
    unnamed x1 -> x0, local copies, waits for them, and re-layouts: 3.16 us -> none
    pallas_call x1, Pallas kernels: 137 us -> 134 us  [fused(): pl.pallas_call(lambda *refs: fused_kernel(steps, strip, length, tm_count,...]
    pallas_call x0 -> x1, Pallas kernels: none -> 2.39 us  [pass_on(): pl.pallas_call(pass_on_kernel, out_shape=jax.ShapeDtypeStruct(flat.shape,...]
where the time goes in v3:
time: 137 us
  Pallas kernels  137 us (100%)
    pallas_call x1, Pallas kernels, fused(): pl.pallas_call(lambda *refs: fused_kernel(steps, strip, length, tm_count,...  134 us

profile of v3, /device:TPU:1, one launch (start us, length us, event | category | flops | bytes accessed | tf_op | source)
XLA Modules:
  0.0 136.9 jit_solution(13522401969124497582)
XLA Ops:
  0.0 134.5 %shard_map.118 = f32[2,256,1024]{2,1,0:T(8,128)} custom-call(f32[256,1024]{1,0:T(8,128)} %refs_0_.1, s32[2,8,8]{2,1,0:T(8,128)} %refs_1_.1, f32[8,128,128]{2,1,0:T(8,128)} %refs_2_.1, s32[8,8]{1,0:T(8,128)} %refs_3_.1, f32[4]{0:T(128)} %refs_4_.1, f32[4]{0:T(128)} %refs_5_.1, f32[1024,128]{1,0:T(8,128)} %constant.16.clone.refs_6_, ...), custom_call_target="tpu_custom_call" | custom-call | tf_op jit(solution)/shard_map/pallas_call | solution.py:1159
  134.5 2.4 %shard_map.119 = f32[512,1024]{1,0:T(8,128)} custom-call(f32[512,1024]{1,0:T(8,128)} %bitcast.2), custom_call_target="tpu_custom_call" | custom-call | tf_op jit(solution)/shard_map/pallas_call | solution.py:1128

commit v4 on v3

--- a/solution.py
+++ b/solution.py
@@ -829,25 +829,35 @@
 
         lax.fori_loop(0, length // LANES, solve, 0)
 
+        def along(i):
+            return jnp.where(y < ys_count // 2, rows_count - 1 - i, i)
+
+        def leave(target):
+            @pl.when(target != r)
+            def _():
+                dy = lax.rem(lax.div(target, 2) + ys_count - y, ys_count)
+                send_y(sweep, j, dy, lax.rem(target + c, 2)).start()
+
         def part(i, _):
             dy, q = lax.rem(lax.div(i, 2) + 1, ys_count), lax.rem(i, 2)
-            target = lax.rem(y + dy, ys_count) * 2 + q
+            target = along(i) if sweep == 0 else lax.rem(y + dy, ys_count) * 2 + q
             rows = rows_at(target * strip, strip)
             out = dot3(s.cth[rows], s.ctl[rows], s.uh[...], s.ul[...])
             s.iy[sweep, j, pl.ds(pl.multiple_of(target * strip + EDGE, EDGE), strip)] = out
             if sweep > 0:
-
-                @pl.when(target != r)
+                leave(target)
+            else:
+
+                @pl.when(i > 0)
                 def _():
-                    send_y(sweep, j, dy, lax.rem(q + c, 2)).start()
+                    leave(along(i - 1))
 
             share(action, sweep, j + 1, i, rows_count)
             return 0
 
         lax.fori_loop(0, rows_count, part, 0)
         if sweep == 0:
-            for dy, dc in peers:
-                send_y(sweep, j, dy, dc).start()
+            leave(along(rows_count - 1))
             s.yr[sweep, j, r] = s.iy[sweep, j, pl.ds(pl.multiple_of(r * strip, EDGE), padded)]
         else:
             mid = pl.ds(pl.multiple_of(r * strip + EDGE, EDGE), strip)
@@ -1060,8 +1070,8 @@
         rows_out(1, 1, relay_away, 0, at_once=True)
 
     by_place(relay_then_rows, rows_then_end)
-    some(pair_up, 1, 1, 0, units)
-    rows_in(1, 0, relay_near)
+    rows_in(1, 0, pair_up)
+    some(relay_near, 1, 1, 0, units)
     some(relay_away, 1, 1, 0, units)
     rows_in(1, 1)
     @pl.when(r < rows_count - 1)

time: 137 us -> 138 us (level)
  no operation moved by 1% of the time
where the time goes in v4:
time: 138 us; the launch traced here: 137 us
  Pallas kernels  137 us (99%)
    pallas_call x1, Pallas kernels, fused(): pl.pallas_call(lambda *refs: fused_kernel(steps, strip, length, tm_count,...  135 us

profile of v4, /device:TPU:1, one launch (start us, length us, event | category | flops | bytes accessed | tf_op | source)
XLA Modules:
  0.0 137.5 jit_solution(16075006586909732813)
XLA Ops:
  0.0 135.1 %shard_map.118 = f32[2,256,1024]{2,1,0:T(8,128)} custom-call(f32[256,1024]{1,0:T(8,128)} %refs_0_.1, s32[2,8,8]{2,1,0:T(8,128)} %refs_1_.1, f32[8,128,128]{2,1,0:T(8,128)} %refs_2_.1, s32[8,8]{1,0:T(8,128)} %refs_3_.1, f32[4]{0:T(128)} %refs_4_.1, f32[4]{0:T(128)} %refs_5_.1, f32[1024,128]{1,0:T(8,128)} %constant.16.clone.refs_6_, ...), custom_call_target="tpu_custom_call" | custom-call | tf_op jit(solution)/shard_map/pallas_call | solution.py:1169
  135.1 2.4 %shard_map.119 = f32[512,1024]{1,0:T(8,128)} custom-call(f32[512,1024]{1,0:T(8,128)} %bitcast.2), custom_call_target="tpu_custom_call" | custom-call | tf_op jit(solution)/shard_map/pallas_call | solution.py:1138

commit v5 on v3

--- a/solution.py
+++ b/solution.py
@@ -272,7 +272,7 @@
 LANES = 128
 EDGE = 8
 ROWS = 32
-UNIT = 64
+UNIT = 128
 MESH = pl.DeviceIdType.MESH
 
 

time: 137 us -> 139 us (1.015)
  Pallas kernels: 137 us -> 139 us
    pallas_call x1, Pallas kernels: 134 us -> 137 us  [fused(): pl.pallas_call(lambda *refs: fused_kernel(steps, strip, length, tm_count,...]
where the time goes in v5:
time: 139 us
  Pallas kernels  139 us (100%)
    pallas_call x1, Pallas kernels, fused(): pl.pallas_call(lambda *refs: fused_kernel(steps, strip, length, tm_count,...  137 us

profile of v5, /device:TPU:1, one launch (start us, length us, event | category | flops | bytes accessed | tf_op | source)
XLA Modules:
  0.0 139.2 jit_solution(10704779089232413088)
XLA Ops:
  0.0 136.8 %shard_map.118 = f32[2,256,1024]{2,1,0:T(8,128)} custom-call(f32[256,1024]{1,0:T(8,128)} %refs_0_.1, s32[2,8,8]{2,1,0:T(8,128)} %refs_1_.1, f32[8,128,128]{2,1,0:T(8,128)} %refs_2_.1, s32[8,8]{1,0:T(8,128)} %refs_3_.1, f32[4]{0:T(128)} %refs_4_.1, f32[4]{0:T(128)} %refs_5_.1, f32[1024,128]{1,0:T(8,128)} %constant.16.clone.refs_6_, ...), custom_call_target="tpu_custom_call" | custom-call | tf_op jit(solution)/shard_map/pallas_call | solution.py:1159
  136.8 2.4 %shard_map.119 = f32[512,1024]{1,0:T(8,128)} custom-call(f32[512,1024]{1,0:T(8,128)} %bitcast.2), custom_call_target="tpu_custom_call" | custom-call | tf_op jit(solution)/shard_map/pallas_call | solution.py:1128
